TPU v7x, 64 devices: a 2x2x8 block of a 4x4x8 slice. The times are simulated.
64 devices in a mesh: rep: 4 (over x, y), dp: 16 (over z, core).
Axes of the slice: x: 2, y: 2, z: 8, core: 2. Of those that a mesh axis runs over, the one named last changes fastest.
The devices are a block of a 4x4x8 slice.
Arguments:
- g_w_gate: bfloat16 [64, 2, 896, 2560], P(('rep', 'dp')), parts along dimension 0
- g_w_up: bfloat16 [64, 2, 896, 2560], P(('rep', 'dp')), parts along dimension 0
- g_w_down: bfloat16 [64, 2, 2560, 896], P(('rep', 'dp')), parts along dimension 0
- w_gate: bfloat16 [2, 896, 2560], replicated
- w_up: bfloat16 [2, 896, 2560], replicated
- w_down: bfloat16 [2, 2560, 896], replicated
- m_w_gate: float32 [2, 896, 2560], P(None, 'dp')
- m_w_up: float32 [2, 896, 2560], P(None, 'dp')
- m_w_down: float32 [2, 2560, 896], P(None, 'dp')
- v_w_gate: float32 [2, 896, 2560], P(None, 'dp')
- v_w_up: float32 [2, 896, 2560], P(None, 'dp')
- v_w_down: float32 [2, 2560, 896], P(None, 'dp')
Outputs:
- output 1: bfloat16 [8, 896, 2560], P('rep'), parts along dimension 0
- output 2: bfloat16 [8, 896, 2560], P('rep'), parts along dimension 0
- output 3: bfloat16 [8, 2560, 896], P('rep'), parts along dimension 0
- output 4: float32 [8, 896, 2560], P('rep', 'dp'), parts along dimension 0
- output 5: float32 [8, 896, 2560], P('rep', 'dp'), parts along dimension 0
- output 6: float32 [8, 2560, 896], P('rep', 'dp'), parts along dimension 0
- output 7: float32 [8, 896, 2560], P('rep', 'dp'), parts along dimension 0
- output 8: float32 [8, 896, 2560], P('rep', 'dp'), parts along dimension 0
- output 9: float32 [8, 2560, 896], P('rep', 'dp'), parts along dimension 0
There are 4 independent parts. A program takes and returns all parts, laid end to end along the dimension named above; an argument that names none is the same for every part.
All inputs are finite; a program needn't handle non-finite values.
Results may differ from a plain program's by a relative error of at most 0.022.
Values are sent between devices in bfloat16 or wider.
A program may use at most 768 MiB of HBM per device.

v0:
```python
import jax
import jax.numpy as jnp
from jax import lax
from jax.sharding import PartitionSpec as P


def adamw(w, m, v, g):
    m = 0.9 * m + 0.1 * g
    v = 0.95 * v + 0.05 * g * g
    step = m * lax.rsqrt(v + 1e-8) + 0.1 * w
    return (w - 0.02 * step).astype(jnp.bfloat16), m, v


def solution(mesh):
    def step(*arrays):
        terms, weights, m, v = (arrays[i : i + 3] for i in (0, 3, 6, 9))
        gradients = [lax.psum_scatter(t[0], "dp", scatter_dimension=1, tiled=True).astype(jnp.float32) for t in terms]
        me = lax.axis_index("dp")
        own = [lax.dynamic_slice_in_dim(w, me * one.shape[1], one.shape[1], 1).astype(jnp.float32) for w, one in zip(weights, m, strict=True)]
        new = [adamw(w, m, v, g) for w, m, v, g in zip(own, m, v, gradients, strict=True)]
        whole = [lax.all_gather(one[0], "dp", axis=1, tiled=True) for one in new]
        return (*whole, *(one[1] for one in new), *(one[2] for one in new))

    all_of, cut = P(None, None, None), P(None, "dp", None)
    return jax.shard_map(
        step,
        mesh=mesh,
        in_specs=(P(("rep", "dp"), None, None, None),) * 3 + (all_of,) * 3 + (cut,) * 6,
        out_specs=(P("rep", None, None),) * 3 + (P("rep", "dp", None),) * 6,
        check_vma=False,
    )
```

profile of v0, /device:TPU:21, one launch (start us, length us, event | category | flops | bytes accessed | tf_op | source)
XLA Modules:
  0.0 427.3 jit_solution(3648039279963816595)
XLA Ops:
  7.2 0.1 reduce-scatter.8.cloned.1.call-start
  7.3 0.7 reduce-scatter.8.cloned.1.call-update
  8.0 0.1 reduce-scatter.10.cloned.1.call-start
  8.1 39.1 %copy.21 = bf16[2,896,2560]{2,0,1:T(2,128)(2,1)} copy(bf16[2,896,2560]{2,1,0:T(8,128)(2,1)} %bitcast.15) | data formatting | bytes 18350080
  47.2 9.6 %copy.25 = bf16[112,8,2,2560]{3,1,2,0:T(8,128)(2,1)} copy(bf16[112,8,2,2560]{3,2,1,0:T(2,128)(2,1)} %bitcast.13) | data formatting | bytes 18350080
  56.8 0.1 reduce-scatter.10.cloned.1.call-update
  56.8 0.1 reduce-scatter.12.cloned.1.call-start
  56.9 39.1 %copy.23 = bf16[2,896,2560]{2,0,1:T(2,128)(2,1)} copy(bf16[2,896,2560]{2,1,0:T(8,128)(2,1)} %bitcast.16) | data formatting | bytes 18350080
  96.0 9.6 %copy.26 = bf16[112,8,2,2560]{3,1,2,0:T(8,128)(2,1)} copy(bf16[112,8,2,2560]{3,2,1,0:T(2,128)(2,1)} %bitcast.14) | data formatting | bytes 18350080
  105.6 0.0 copy-start
  105.6 0.0 copy-start.1
  105.6 0.1 reduce-scatter.12.cloned.1.call-update
  105.7 0.1 all-gather.8.cloned.1.call-start
  105.7 0.0 reduce-scatter.8.cloned.1.call-done
  105.8 1.1 copy-done
  106.8 0.3 copy-done.1
  107.2 0.0 copy-start.3
  107.2 3.2 fusion.10
  110.4 0.0 copy-start.2
  110.4 0.1 all-gather.8.cloned.1.call-update
  110.5 0.1 all-gather.4.cloned.1.call-start
  110.5 41.6 %reduce-scatter.10.cloned.1.call-done = bf16[56,5120]{1,0:T(8,128)(2,1)} async-done(((bf16[896,5120]{1,0:T(8,128)(2,1)}), bf16[56,5120]{1,0:T(8,128)(2,1)}) %reduce-scatter.10.cloned.1.call-update) | async-done | bytes 573456
  152.1 1.5 reshape.19
  153.6 0.0 copy-done.3
  153.6 0.0 copy-done.2
  153.6 2.9 fusion.2
  156.5 0.0 copy-start.4
  156.6 0.1 all-gather.4.cloned.1.call-update
  156.6 0.2 all-gather.6.cloned.1.call-start
  156.9 66.2 %reduce-scatter.12.cloned.1.call-done = bf16[56,5120]{1,0:T(8,128)(2,1)} async-done(((bf16[896,5120]{1,0:T(8,128)(2,1)}), bf16[56,5120]{1,0:T(8,128)(2,1)}) %reduce-scatter.12.cloned.1.call-update) | async-done | bytes 573456
  223.0 1.5 reshape.21
  224.5 0.0 copy-done.4
  224.5 3.3 fusion.6
  227.8 0.1 all-gather.6.cloned.1.call-update
  227.9 55.2 %all-gather.8.cloned.1.call-done = bf16[2,2560,896]{2,1,0:T(8,128)(2,1)} async-done(((bf16[2,160,896]{2,1,0:T(8,128)(2,1)}), bf16[2,2560,896]{2,1,0:T(8,128)(2,1)}) %all-gather.8.cloned.1.call-update) | async-done | bytes 9175056 | tf_op jit(solution)/shard_map/all_gather | solution.py:21
  283.1 56.8 %all-gather.4.cloned.1.call-done = bf16[2,896,2560]{2,1,0:T(8,128)(2,1)} async-done(((bf16[2,56,2560]{2,1,0:T(8,128)(2,1)}), bf16[2,896,2560]{2,1,0:T(8,128)(2,1)}) %all-gather.4.cloned.1.call-update) | async-done | bytes 9175056 | tf_op jit(solution)/shard_map/all_gather | solution.py:21
  339.9 56.8 %all-gather.6.cloned.1.call-done = bf16[2,896,2560]{2,1,0:T(8,128)(2,1)} async-done(((bf16[2,56,2560]{2,1,0:T(8,128)(2,1)}), bf16[2,896,2560]{2,1,0:T(8,128)(2,1)}) %all-gather.6.cloned.1.call-update) | async-done | bytes 9175056 | tf_op jit(solution)/shard_map/all_gather | solution.py:21
  396.8 7.8 %copy.38 = bf16[2,896,2560]{2,1,0:T(8,128)(2,1)} copy(bf16[2,896,2560]{2,1,0:T(8,128)(2,1)} %all-gather.4.cloned.1.call-done) | data formatting | bytes 18350080
  404.6 7.8 %copy.39 = bf16[2,896,2560]{2,1,0:T(8,128)(2,1)} copy(bf16[2,896,2560]{2,1,0:T(8,128)(2,1)} %all-gather.6.cloned.1.call-done) | data formatting | bytes 18350080
  412.5 8.0 %copy.40 = bf16[2,2560,896]{2,1,0:T(8,128)(2,1)} copy(bf16[2,2560,896]{2,1,0:T(8,128)(2,1)} %all-gather.8.cloned.1.call-done) | data formatting | bytes 18350080
Async XLA Ops:
  7.2 98.6 %reduce-scatter.8.cloned.1.call-start = ((), (), s32[]{:S(2)}) async-start(), calls=%async_computation.5 | async-start | bytes 9748480 | tf_op jit(solution)/shard_map/reduce_scatter | solution.py:17
  8.0 144.1 %reduce-scatter.10.cloned.1.call-start = ((), (), s32[]{:S(2)}) async-start(), calls=%async_computation.7 | async-start | bytes 9748480
  56.8 166.2 %reduce-scatter.12.cloned.1.call-start = ((), (), s32[]{:S(2)}) async-start(), calls=%async_computation.8 | async-start | bytes 9748480
  105.6 1.3 copy-start
  105.6 1.6 copy-start.1
  105.7 177.4 %all-gather.8.cloned.1.call-start = ((), (), s32[]{:S(2)}) async-start(), calls=%async_computation.6 | async-start | bytes 9748480 | tf_op jit(solution)/shard_map/all_gather | solution.py:21
  107.2 46.4 %copy-start.3 = (f32[2,56,2560]{2,1,0:T(8,128)S(1)}, f32[2,56,2560]{2,1,0:T(8,128)}, u32[]{:S(2)}) copy-start(f32[2,56,2560]{2,1,0:T(8,128)} %param.18) | copy-start | bytes 3440644
  110.4 43.2 %copy-start.2 = (f32[2,56,2560]{2,1,0:T(8,128)S(1)}, f32[2,56,2560]{2,1,0:T(8,128)}, u32[]{:S(2)}) copy-start(f32[2,56,2560]{2,1,0:T(8,128)} %param.21) | copy-start | bytes 3440644
  110.5 229.5 %all-gather.4.cloned.1.call-start = ((), (), s32[]{:S(2)}) async-start(), calls=%async_computation.3 | async-start | bytes 9748480 | tf_op jit(solution)/shard_map/all_gather | solution.py:21
  156.5 68.0 %copy-start.4 = (f32[2,56,2560]{2,1,0:T(8,128)S(1)}, f32[2,56,2560]{2,1,0:T(8,128)}, u32[]{:S(2)}) copy-start(f32[2,56,2560]{2,1,0:T(8,128)} %param.22) | copy-start | bytes 3440644
  156.6 240.2 %all-gather.6.cloned.1.call-start = ((), (), s32[]{:S(2)}) async-start(), calls=%async_computation.4 | async-start | bytes 9748480 | tf_op jit(solution)/shard_map/all_gather | solution.py:21
Sparse Core Ops, SparseCore 0:
  10.4 70.8 reduce-scatter.7
  84.3 67.7 reduce-scatter.9
  155.1 67.9 reduce-scatter.11
  224.5 58.5 all-gather.7
  285.2 54.7 all-gather.3
  342.0 54.7 all-gather.5
where the time goes:
time: 428 us; the launch traced here: 427 us
  waiting for transfers between devices  278 us (65%)
  local copies, waits for them, and re-layouts  125 us (29%)
  between operations  14.2 us (3%)
  other arithmetic  9.46 us (2%)
    all_gather x3, waiting for transfers between devices, step(): whole = [lax.all_gather(one[0], 'dp', axis=1, tiled=True) for one in new]  169 us
    unnamed x19, local copies, waits for them, and re-layouts  125 us
    unnamed x8, waiting for transfers between devices  109 us
    convert_element_type x3, other arithmetic, adamw(): return ((w - 0.02 * step).astype(jnp.bfloat16), m, v)  9.46 us
  transfers between devices with their start and end apart: 6, of which 5 were waited for; matrix products, arithmetic and copies ran while one was open for 26% of the time, Pallas kernels for 0%

commit v1 on v0

v1 whole, which is shorter than its diff:
```python
import functools

import jax
import jax.numpy as jnp
from jax import lax
from jax.experimental import pallas as pl
from jax.experimental.pallas import tpu as pltpu
from jax.sharding import PartitionSpec as P

CORES = 2
SUBLANES = 8
VMEM_LIMIT = 20 * 2**20


def adamw(w, m, v, g):
    m = 0.9 * m + 0.1 * g
    v = 0.95 * v + 0.05 * g * g
    step = m * lax.rsqrt(v + 1e-8) + 0.1 * w
    return (w - 0.02 * step).astype(jnp.bfloat16), m, v


def kernel(n, units, *refs):
    g, w, m_in, v_in, out, m, v = (refs[i * units : (i + 1) * units] for i in range(7))
    own, part, w_own = (refs[i * units : (i + 1) * units] for i in (7, 8, 9))
    g = refs[:units]
    scratch = refs[10 * units :]
    own_sem, state_sem, push_send, push_recv, sum_send, sum_recv, new_send, new_recv, pass_send, pass_recv = scratch

    me = lax.axis_index("dp")
    z, core = me // CORES, me % CORES
    ring = n // CORES
    partner = z * CORES + 1 - core
    last = ring - 1
    ways = (1, -1)

    def chip(offset):
        return lax.rem(z + offset + 2 * ring, ring)

    def owner(d, k):
        return chip(-ways[d] * (k + 1))

    def to(index):
        return {"device_id": {"dp": index}, "device_id_type": pl.DeviceIdType.MESH}

    def following(d):
        return to(chip(ways[d]) * CORES + core)

    def load_own(d, k, u):
        slot = lax.rem(k, 2)
        return pltpu.make_async_copy(g[u].at[d, owner(d, k) * CORES + core], own[u].at[slot, d], own_sem.at[slot, d, u])

    def push(d, k, u):
        return pltpu.make_async_remote_copy(
            g[u].at[d, owner(d, k) * CORES + 1 - core], part[u].at[d, k], push_send.at[d, k, u], push_recv.at[d, k, u], **to(partner)
        )

    def send_sum(d, k, u):
        block = out[u].at[d, owner(d, k) * CORES + core]
        return pltpu.make_async_remote_copy(block, block, sum_send.at[d, k, u], sum_recv.at[d, k, u], **following(d))

    def send_new(d, j, u):
        block = out[u].at[d, chip(-ways[d] * j) * CORES + core]
        return pltpu.make_async_remote_copy(block, block, new_send.at[d, j, u], new_recv.at[d, j, u], **following(d))

    def pass_new(d, j, u):
        block = out[u].at[d, chip(-ways[d] * j) * CORES + core]
        return pltpu.make_async_remote_copy(block, block, pass_send.at[d, j, u], pass_recv.at[d, j, u], **to(partner))

    def load_state(d, u):
        return (
            pltpu.make_async_copy(w[u].at[d, me], w_own[u].at[d], state_sem.at[0, d, u]),
            pltpu.make_async_copy(m_in[u].at[d], m[u].at[d], state_sem.at[1, d, u]),
            pltpu.make_async_copy(v_in[u].at[d], v[u].at[d], state_sem.at[2, d, u]),
        )

    every = [(u, d) for u in range(units) for d in range(2)]

    for u, d in every:
        load_own(d, 0, u).start()

    barrier = pltpu.get_barrier_semaphore()
    for index in (chip(1) * CORES + core, chip(-1) * CORES + core, partner):
        pl.semaphore_signal(barrier, inc=1, **to(index))
    pl.semaphore_wait(barrier, 3)

    for k in (0, 1):
        for u, d in every:
            push(d, k, u).start()

    def add(d, k, u, arrived):
        slot, block = lax.rem(k, 2), owner(d, k) * CORES + core
        load_own(d, k, u).wait()
        push(d, k, u).wait_recv()

        @pl.loop(0, own[u].shape[2])
        def _(row):
            total = own[u][slot, d, row].astype(jnp.float32) + part[u][d, k, row].astype(jnp.float32)
            if arrived:
                total = out[u][d, block, row].astype(jnp.float32) + total
            out[u][d, block, row] = total.astype(out[u].dtype)

    for u, d in every:
        load_own(d, 1, u).start()
    for u, d in every:
        add(d, 0, u, False)
        send_sum(d, 0, u).start()
    for u, d in every:
        for copy in load_state(d, u):
            copy.start()

    @pl.loop(1, last)
    def _(k):
        for u, d in every:
            load_own(d, k + 1, u).start()
            push(d, k + 1, u).start()
        for u, d in every:
            send_sum(d, k - 1, u).wait_recv()
            add(d, k, u, True)
            send_sum(d, k - 1, u).wait_send()
            send_sum(d, k, u).start()

    for u, d in every:
        slot = last % 2
        load_own(d, last, u).wait()
        push(d, last, u).wait_recv()
        for copy in load_state(d, u):
            copy.wait()
        send_sum(d, last - 1, u).wait_recv()

        @pl.loop(0, own[u].shape[2])
        def _(row):
            total = own[u][slot, d, row].astype(jnp.float32) + part[u][d, last, row].astype(jnp.float32)
            total = out[u][d, me, row].astype(jnp.float32) + total
            gradient = total.astype(jnp.bfloat16).astype(jnp.float32)
            new = adamw(w_own[u][d, row].astype(jnp.float32), m[u][d, row], v[u][d, row], gradient)
            out[u][d, me, row], m[u][d, row], v[u][d, row] = new

        send_sum(d, last - 1, u).wait_send()
        send_new(d, 0, u).start()
        pass_new(d, 0, u).start()

    @pl.loop(1, last)
    def _(j):
        for u, d in every:
            send_new(d, j - 1, u).wait_recv()
            send_new(d, j, u).start()
            pass_new(d, j, u).start()

    for u, d in every:
        send_new(d, last - 1, u).wait_recv()
        pass_new(d, last, u).start()

    @pl.loop(0, ring)
    def _(j):
        for u, d in every:
            push(d, j, u).wait_send()
            pass_new(d, j, u).wait()

    @pl.loop(0, last)
    def _(j):
        for u, d in every:
            send_new(d, j, u).wait_send()


def place(*refs):
    count = (len(refs) - 1) // 2
    copies = [pltpu.make_async_copy(refs[i], refs[count + i], refs[-1].at[i]) for i in range(count)]
    for copy in copies:
        copy.start()
    for copy in copies:
        copy.wait()


def solution(mesh):
    n = mesh.shape["dp"]

    def step(*arrays):
        terms, weights, m, v = (arrays[i : i + 3] for i in (0, 3, 6, 9))
        units = len(terms)
        layers = weights[0].shape[0]

        def blocks(x, count):
            return x.reshape(layers, *([count] if count else []), -1, SUBLANES, x.shape[-1])

        terms = [blocks(t[0], n) for t in terms]
        weights_in = [blocks(x, n) for x in weights]
        m_in = [blocks(x, 0) for x in m]
        v_in = [blocks(x, 0) for x in v]
        ring = n // CORES
        block = [x.shape[1:] for x in m_in]
        dma = lambda *shape: pltpu.SemaphoreType.DMA(shape)
        new = pl.pallas_call(
            functools.partial(kernel, n, units),
            out_shape=[pltpu.VMEM(x.shape, x.dtype) for x in (*weights_in, *m_in, *v_in)],
            in_specs=[pl.BlockSpec(memory_space=pltpu.HBM)] * (4 * units),
            out_specs=[pl.BlockSpec(memory_space=pltpu.VMEM)] * (3 * units),
            scratch_shapes=[
                *(pltpu.VMEM((2, 2, *b), jnp.bfloat16) for b in block),
                *(pltpu.VMEM((2, ring, *b), jnp.bfloat16) for b in block),
                *(pltpu.VMEM((2, *b), jnp.bfloat16) for b in block),
                dma(2, 2, units),
                dma(3, 2, units),
                *[dma(2, ring, units) for _ in range(8)],
            ],
            compiler_params=pltpu.CompilerParams(collective_id=0, has_side_effects=True, vmem_limit_bytes=VMEM_LIMIT),
            name="step_end",
        )(*(pltpu.with_memory_space_constraint(x, pltpu.HBM) for x in (*terms, *weights_in, *m_in, *v_in)))
        new = pl.pallas_call(
            place,
            out_shape=[jax.ShapeDtypeStruct(x.shape, x.dtype) for x in new],
            in_specs=[pl.BlockSpec(memory_space=pltpu.VMEM)] * len(new),
            out_specs=[pl.BlockSpec(memory_space=pltpu.HBM)] * len(new),
            scratch_shapes=[dma(len(new))],
            compiler_params=pltpu.CompilerParams(vmem_limit_bytes=VMEM_LIMIT),
            name="place",
        )(*(pltpu.with_memory_space_constraint(x, pltpu.VMEM) for x in new))
        return tuple(x.reshape(like.shape) for x, like in zip(new, (*weights, *m, *v), strict=True))

    all_of, cut = P(None, None, None), P(None, "dp", None)
    return jax.shard_map(
        step,
        mesh=mesh,
        in_specs=(P(("rep", "dp"), None, None, None),) * 3 + (all_of,) * 3 + (cut,) * 6,
        out_specs=(P("rep", None, None),) * 3 + (P("rep", "dp", None),) * 6,
        check_vma=False,
    )
```

time: 428 us -> 287 us (0.67)
  Pallas kernels: 0 us -> 287 us
  waiting for transfers between devices: 278 us -> 0 us
  local copies, waits for them, and re-layouts: 125 us -> 0 us
  between operations: 14.2 us -> 0.65 us
  other arithmetic: 9.46 us -> 0 us
    pallas_call x0 -> x2, Pallas kernels: none -> 287 us  [the longest x1 275 us: step(): pl.pallas_call(functools.partial(kernel, n, units), out_shape=[pltpu.VMEM...]
    all_gather x3 -> x0, waiting for transfers between devices: 169 us -> none  [step(): whole = [lax.all_gather(one[0], 'dp', axis=1, tiled=True) for one in new]]
    unnamed x19 -> x0, local copies, waits for them, and re-layouts: 125 us -> none
    unnamed x8 -> x0, waiting for transfers between devices: 109 us -> none
    convert_element_type x3 -> x0, other arithmetic: 9.46 us -> none  [adamw(): return ((w - 0.02 * step).astype(jnp.bfloat16), m, v)]
  transfers between devices with their start and end apart: 6 -> 0, of which waited for: 5 -> 0; matrix products, arithmetic and copies ran while one was open for 26% -> 0% of each run, Pallas kernels for 0% -> 0%
where the time goes in v1:
time: 287 us
  Pallas kernels  287 us (100%)
    pallas_call x1, Pallas kernels, step(): pl.pallas_call(functools.partial(kernel, n, units), out_shape=[pltpu.VMEM...  275 us
    pallas_call x1, Pallas kernels, step(): pl.pallas_call(place, out_shape=[jax.ShapeDtypeStruct(x.shape, x.dtype) f...  11.4 us

profile of v1, /device:TPU:21, one launch (start us, length us, event | category | flops | bytes accessed | tf_op | source)
XLA Modules:
  0.0 287.3 jit_solution(17789550541822542456)
XLA Ops:
  0.6 275.3 %step_end.1 = (bf16[2,16,7,8,2560]{4,3,2,1,0:T(8,128)(2,1)S(1)}, bf16[2,16,7,8,2560]{4,3,2,1,0:T(8,128)(2,1)S(1)}, bf16[2,16,20,8,896]{4,3,2,1,0:T(8,128)(2,1)S(...) custom-call(bf16[2,16,7,8,2560]{4,3,2,1,0:T(8,128)(2,1)} %bitcast.21, ...), custom_call_target="tpu_custom_call" | custom-call | tf_op jit(solution)/shard_map/step_end/pallas_call | solution.py:192
  275.9 11.4 %place.1 = (bf16[2,16,7,8,2560]{4,3,2,1,0:T(8,128)(2,1)}, bf16[2,16,7,8,2560]{4,3,2,1,0:T(8,128)(2,1)}, bf16[2,16,20,8,896]{4,3,2,1,0:T(8,128)(2,1)}, f32[2,7,8,...) custom-call(bf16[2,16,7,8,2560]{4,3,2,1,0:T(8,128)(2,1)S(1)} %get-tu, ...), custom_call_target="tpu_custom_call" | custom-call | tf_op jit(solution)/shard_map/place/pallas_call | solution.py:208

commit v2 on v0

v2 whole, which is shorter than its diff:
```python
import functools

import jax
import jax.numpy as jnp
from jax import lax
from jax.experimental import pallas as pl
from jax.experimental.pallas import tpu as pltpu
from jax.sharding import PartitionSpec as P

CORES = 2
SUBLANES = 8
VMEM_LIMIT = 20 * 2**20


def adamw(w, m, v, g):
    m = 0.9 * m + 0.1 * g
    v = 0.95 * v + 0.05 * g * g
    step = m * lax.rsqrt(v + 1e-8) + 0.1 * w
    return (w - 0.02 * step).astype(jnp.bfloat16), m, v


def cuts(rows):
    a = max(rows // 8, 1)
    b = max(rows // 3, a + 1)
    return (0, a), (a, b - a), (b, rows - b)


def kernel(n, units, *refs):
    g, w, m_in, v_in, out, m, v, own, part, w_own = (refs[i * units : (i + 1) * units] for i in range(10))
    own_sem, state_sem, push_send, push_recv, ring_send, ring_recv, pass_send, pass_recv, first_recv, tail_recv = refs[10 * units :]

    me = lax.axis_index("dp")
    z, core = me // CORES, me % CORES
    ring = n // CORES
    partner = z * CORES + 1 - core
    last = ring - 1
    ways = (0, 1)
    final = units - 1

    def chip(offset):
        return lax.rem(z + offset + 2 * ring, ring)

    def behind(d, j):
        return chip(j if d else -j)

    def owner(d, k):
        return behind(d, k + 1)

    def to(index):
        return {"device_id": {"dp": index}, "device_id_type": pl.DeviceIdType.MESH}

    def following(d):
        return to(behind(d, -1) * CORES + core)

    def wait_bytes(ref, sem):
        pltpu.make_async_copy(ref, ref, sem).wait()

    def load_own(k, u):
        slot = lax.rem(k, 2)
        for d in ways:
            pltpu.make_async_copy(g[u].at[d, owner(d, k) * CORES + core], own[u].at[slot, d], own_sem.at[slot, u]).start()

    def push(d, k, u, sem, rows=slice(None)):
        pltpu.make_async_remote_copy(
            g[u].at[d, owner(d, k) * CORES + 1 - core, rows], part[u].at[d, k, rows], push_send.at[d, u], sem, **to(partner)
        ).start()

    def push_all(k, u):
        for d in ways:
            push(d, k, u, push_recv.at[k, u])

    def terms_here(k, u):
        wait_bytes(own[u].at[lax.rem(k, 2)], own_sem.at[lax.rem(k, 2), u])
        wait_bytes(part[u].at[:, k], push_recv.at[k, u])

    def send(block, d, t, u, rows=slice(None), sem=None):
        piece = out[u].at[d, block, rows]
        sem = ring_recv.at[lax.rem(t, 3), d, u] if sem is None else sem
        pltpu.make_async_remote_copy(piece, piece, ring_send.at[d, u], sem, **following(d)).start()

    def sent(d, u):
        wait_bytes(out[u].at[d, 0], ring_send.at[d, u])

    def arrived(block, d, t, u):
        wait_bytes(out[u].at[d, block], ring_recv.at[lax.rem(t, 3), d, u])

    def pass_on(block, d, u, rows=slice(None)):
        piece = out[u].at[d, block, rows]
        pltpu.make_async_remote_copy(piece, piece, pass_send.at[d, u], pass_recv.at[d, u], **to(partner)).start()

    def terms(slot, d, k, u, row):
        return own[u][slot, d, row].astype(jnp.float32) + part[u][d, k, row].astype(jnp.float32)

    rows_of = [x.shape[2] for x in own]

    for u in range(units):
        load_own(0, u)

    barrier = pltpu.get_barrier_semaphore()
    for index in (chip(1) * CORES + core, chip(-1) * CORES + core, partner):
        pl.semaphore_signal(barrier, inc=1, **to(index))
    pl.semaphore_wait(barrier, 3)

    for p, (at, count) in enumerate(cuts(rows_of[0])):
        for d in ways:
            push(d, 0, 0, first_recv.at[d, p], pl.ds(at, count))
    for u in range(1, units):
        push_all(0, u)
    for u in range(units):
        load_own(1, u)
        push_all(1, u)

    def begin(d, u, at, count):
        block = owner(d, 0) * CORES + core

        @pl.loop(at, at + count)
        def _(row):
            out[u][d, block, row] = terms(0, d, 0, u, row).astype(out[u].dtype)

        send(block, d, 0, u, pl.ds(at, count))

    wait_bytes(own[0].at[0], own_sem.at[0, 0])
    for p, (at, count) in enumerate(cuts(rows_of[0])):
        for d in ways:
            wait_bytes(part[0].at[d, 0, pl.ds(at, count)], first_recv.at[d, p])
            begin(d, 0, at, count)
    for u in range(1, units):
        terms_here(0, u)
        for d in ways:
            begin(d, u, 0, rows_of[u])

    state = []
    for u in range(units):
        state.append(
            (
                pltpu.make_async_copy(w[u].at[:, me], w_own[u], state_sem.at[0, u]),
                pltpu.make_async_copy(m_in[u], m[u], state_sem.at[1, u]),
                pltpu.make_async_copy(v_in[u], v[u], state_sem.at[2, u]),
            )
        )
        for copy in state[u]:
            copy.start()

    @pl.loop(1, last)
    def _(k):
        slot = lax.rem(k, 2)
        for u in range(units):
            load_own(k + 1, u)
            push_all(k + 1, u)
        for u in range(units):
            terms_here(k, u)
            for d in ways:
                block = owner(d, k) * CORES + core
                arrived(block, d, k - 1, u)

                @pl.loop(0, rows_of[u])
                def _(row):
                    total = out[u][d, block, row].astype(jnp.float32) + terms(slot, d, k, u, row)
                    out[u][d, block, row] = total.astype(out[u].dtype)

                sent(d, u)
                send(block, d, k, u)

    for u in range(units):
        terms_here(last, u)
        for copy in state[u]:
            copy.wait()
        for d in ways:
            arrived(me, d, last - 1, u)

            @pl.loop(0, rows_of[u])
            def _(row):
                total = out[u][d, me, row].astype(jnp.float32) + terms(last % 2, d, last, u, row)
                gradient = total.astype(jnp.bfloat16).astype(jnp.float32)
                new = adamw(w_own[u][d, row].astype(jnp.float32), m[u][d, row], v[u][d, row], gradient)
                out[u][d, me, row], m[u][d, row], v[u][d, row] = new

            sent(d, u)
            send(me, d, last, u)
            pass_on(me, d, u)

    @pl.loop(1, last - 1)
    def _(j):
        for u in range(units):
            for d in ways:
                block = behind(d, j) * CORES + core
                arrived(block, d, last + j - 1, u)
                sent(d, u)
                send(block, d, last + j, u)
                pass_on(block, d, u)

    for u in range(units):
        for d in ways:
            block = behind(d, last - 1) * CORES + core
            arrived(block, d, 2 * last - 2, u)
            sent(d, u)
            if u == final:
                for p, (at, count) in enumerate(cuts(rows_of[u])[::-1]):
                    send(block, d, 2 * last - 1, u, pl.ds(at, count), tail_recv.at[d, p])
            else:
                send(block, d, 2 * last - 1, u)
            pass_on(block, d, u)

    for u in range(final):
        for d in ways:
            block = behind(d, last) * CORES + core
            arrived(block, d, 2 * last - 1, u)
            pass_on(block, d, u)
    for p, (at, count) in enumerate(cuts(rows_of[final])[::-1]):
        for d in ways:
            block = behind(d, last) * CORES + core
            wait_bytes(out[final].at[d, block, pl.ds(at, count)], tail_recv.at[d, p])
            pass_on(block, d, final, pl.ds(at, count))

    for u in range(units):
        for d in ways:
            sent(d, u)
            wait_bytes(part[u].at[d], push_send.at[d, u])
            wait_bytes(out[u].at[d, pl.ds(0, ring)], pass_send.at[d, u])
            wait_bytes(out[u].at[d, pl.ds(0, ring)], pass_recv.at[d, u])


def place(*refs):
    count = (len(refs) - 1) // 2
    copies = [pltpu.make_async_copy(refs[i], refs[count + i], refs[-1].at[i]) for i in range(count)]
    for copy in copies:
        copy.start()
    for copy in copies:
        copy.wait()


def solution(mesh):
    n = mesh.shape["dp"]

    def step(*arrays):
        terms, weights, m, v = (arrays[i : i + 3] for i in (0, 3, 6, 9))
        units = len(terms)
        layers = weights[0].shape[0]

        def blocks(x, count):
            return x.reshape(layers, *([count] if count else []), -1, SUBLANES, x.shape[-1])

        terms = [blocks(t[0], n) for t in terms]
        weights_in = [blocks(x, n) for x in weights]
        m_in = [blocks(x, 0) for x in m]
        v_in = [blocks(x, 0) for x in v]
        ring = n // CORES
        block = [x.shape[1:] for x in m_in]
        dma = lambda *shape: pltpu.SemaphoreType.DMA(shape)
        new = pl.pallas_call(
            functools.partial(kernel, n, units),
            out_shape=[pltpu.VMEM(x.shape, x.dtype) for x in (*weights_in, *m_in, *v_in)],
            in_specs=[pl.BlockSpec(memory_space=pltpu.HBM)] * (4 * units),
            out_specs=[pl.BlockSpec(memory_space=pltpu.VMEM)] * (3 * units),
            scratch_shapes=[
                *(pltpu.VMEM((2, 2, *b), jnp.bfloat16) for b in block),
                *(pltpu.VMEM((2, ring, *b), jnp.bfloat16) for b in block),
                *(pltpu.VMEM((2, *b), jnp.bfloat16) for b in block),
                dma(2, units),
                dma(3, units),
                dma(2, units),
                dma(ring, units),
                dma(2, units),
                dma(3, 2, units),
                dma(2, units),
                dma(2, units),
                dma(2, 3),
                dma(2, 3),
            ],
            compiler_params=pltpu.CompilerParams(collective_id=0, has_side_effects=True, vmem_limit_bytes=VMEM_LIMIT),
            name="step_end",
        )(*(pltpu.with_memory_space_constraint(x, pltpu.HBM) for x in (*terms, *weights_in, *m_in, *v_in)))
        new = pl.pallas_call(
            place,
            out_shape=[jax.ShapeDtypeStruct(x.shape, x.dtype) for x in new],
            in_specs=[pl.BlockSpec(memory_space=pltpu.VMEM)] * len(new),
            out_specs=[pl.BlockSpec(memory_space=pltpu.HBM)] * len(new),
            scratch_shapes=[dma(len(new))],
            compiler_params=pltpu.CompilerParams(vmem_limit_bytes=VMEM_LIMIT),
            name="place",
        )(*(pltpu.with_memory_space_constraint(x, pltpu.VMEM) for x in new))
        return tuple(x.reshape(like.shape) for x, like in zip(new, (*weights, *m, *v), strict=True))

    all_of, cut = P(None, None, None), P(None, "dp", None)
    return jax.shard_map(
        step,
        mesh=mesh,
        in_specs=(P(("rep", "dp"), None, None, None),) * 3 + (all_of,) * 3 + (cut,) * 6,
        out_specs=(P("rep", None, None),) * 3 + (P("rep", "dp", None),) * 6,
        check_vma=False,
    )
```

time: 428 us -> 283 us (0.66)
  Pallas kernels: 0 us -> 283 us
  waiting for transfers between devices: 278 us -> 0 us
  local copies, waits for them, and re-layouts: 125 us -> 0 us
  between operations: 14.2 us -> 0.65 us
  other arithmetic: 9.46 us -> 0 us
    pallas_call x0 -> x2, Pallas kernels: none -> 283 us  [the longest x1 271 us: step(): pl.pallas_call(functools.partial(kernel, n, units), out_shape=[pltpu.VMEM...]
    all_gather x3 -> x0, waiting for transfers between devices: 169 us -> none  [step(): whole = [lax.all_gather(one[0], 'dp', axis=1, tiled=True) for one in new]]
    unnamed x19 -> x0, local copies, waits for them, and re-layouts: 125 us -> none
    unnamed x8 -> x0, waiting for transfers between devices: 109 us -> none
    convert_element_type x3 -> x0, other arithmetic: 9.46 us -> none  [adamw(): return ((w - 0.02 * step).astype(jnp.bfloat16), m, v)]
  transfers between devices with their start and end apart: 6 -> 0, of which waited for: 5 -> 0; matrix products, arithmetic and copies ran while one was open for 26% -> 0% of each run, Pallas kernels for 0% -> 0%
where the time goes in v2:
time: 283 us
  Pallas kernels  283 us (100%)
    pallas_call x1, Pallas kernels, step(): pl.pallas_call(functools.partial(kernel, n, units), out_shape=[pltpu.VMEM...  271 us
    pallas_call x1, Pallas kernels, step(): pl.pallas_call(place, out_shape=[jax.ShapeDtypeStruct(x.shape, x.dtype) f...  11.4 us

profile of v2, /device:TPU:21, one launch (start us, length us, event | category | flops | bytes accessed | tf_op | source)
XLA Modules:
  0.0 283.2 jit_solution(10722700908216643988)
XLA Ops:
  0.6 271.2 %step_end.1 = (bf16[2,16,7,8,2560]{4,3,2,1,0:T(8,128)(2,1)S(1)}, bf16[2,16,7,8,2560]{4,3,2,1,0:T(8,128)(2,1)S(1)}, bf16[2,16,20,8,896]{4,3,2,1,0:T(8,128)(2,1)S(...) custom-call(bf16[2,16,7,8,2560]{4,3,2,1,0:T(8,128)(2,1)} %bitcast.21, ...), custom_call_target="tpu_custom_call" | custom-call | tf_op jit(solution)/shard_map/step_end/pallas_call | solution.py:250
  271.8 11.4 %place.1 = (bf16[2,16,7,8,2560]{4,3,2,1,0:T(8,128)(2,1)}, bf16[2,16,7,8,2560]{4,3,2,1,0:T(8,128)(2,1)}, bf16[2,16,20,8,896]{4,3,2,1,0:T(8,128)(2,1)}, f32[2,7,8,...) custom-call(bf16[2,16,7,8,2560]{4,3,2,1,0:T(8,128)(2,1)S(1)} %get-tu, ...), custom_call_target="tpu_custom_call" | custom-call | tf_op jit(solution)/shard_map/place/pallas_call | solution.py:273

commit v3 on v2

--- a/solution.py
+++ b/solution.py
@@ -25,9 +25,12 @@
     return (0, a), (a, b - a), (b, rows - b)
 
 
-def kernel(n, units, *refs):
-    g, w, m_in, v_in, out, m, v, own, part, w_own = (refs[i * units : (i + 1) * units] for i in range(10))
-    own_sem, state_sem, push_send, push_recv, ring_send, ring_recv, pass_send, pass_recv, first_recv, tail_recv = refs[10 * units :]
+def kernel(n, order, late, *refs):
+    units = len(order)
+    g, w, m_in, v_in, out, m, v = (refs[i * units : (i + 1) * units] for i in range(7))
+    after, refs = refs[7 * units : 7 * units + 2], refs[7 * units + 2 :]
+    own, part, w_own = (refs[i * units : (i + 1) * units] for i in range(3))
+    own_sem, state_sem, push_send, push_recv, ring_send, ring_recv, pass_send, pass_recv, first_recv, tail_recv = refs[3 * units :]
 
     me = lax.axis_index("dp")
     z, core = me // CORES, me % CORES
@@ -35,7 +38,7 @@
     partner = z * CORES + 1 - core
     last = ring - 1
     ways = (0, 1)
-    final = units - 1
+    lead, *others = order
 
     def chip(offset):
         return lax.rem(z + offset + 2 * ring, ring)
@@ -93,7 +96,7 @@
 
     rows_of = [x.shape[2] for x in own]
 
-    for u in range(units):
+    for u in order:
         load_own(0, u)
 
     barrier = pltpu.get_barrier_semaphore()
@@ -101,12 +104,12 @@
         pl.semaphore_signal(barrier, inc=1, **to(index))
     pl.semaphore_wait(barrier, 3)
 
-    for p, (at, count) in enumerate(cuts(rows_of[0])):
-        for d in ways:
-            push(d, 0, 0, first_recv.at[d, p], pl.ds(at, count))
-    for u in range(1, units):
+    for p, (at, count) in enumerate(cuts(rows_of[lead])):
+        for d in ways:
+            push(d, 0, lead, first_recv.at[d, p], pl.ds(at, count))
+    for u in others:
         push_all(0, u)
-    for u in range(units):
+    for u in order:
         load_own(1, u)
         push_all(1, u)
 
@@ -119,24 +122,22 @@
 
         send(block, d, 0, u, pl.ds(at, count))
 
-    wait_bytes(own[0].at[0], own_sem.at[0, 0])
-    for p, (at, count) in enumerate(cuts(rows_of[0])):
-        for d in ways:
-            wait_bytes(part[0].at[d, 0, pl.ds(at, count)], first_recv.at[d, p])
-            begin(d, 0, at, count)
-    for u in range(1, units):
+    wait_bytes(own[lead].at[0], own_sem.at[0, lead])
+    for p, (at, count) in enumerate(cuts(rows_of[lead])):
+        for d in ways:
+            wait_bytes(part[lead].at[d, 0, pl.ds(at, count)], first_recv.at[d, p])
+            begin(d, lead, at, count)
+    for u in others:
         terms_here(0, u)
         for d in ways:
             begin(d, u, 0, rows_of[u])
 
-    state = []
-    for u in range(units):
-        state.append(
-            (
-                pltpu.make_async_copy(w[u].at[:, me], w_own[u], state_sem.at[0, u]),
-                pltpu.make_async_copy(m_in[u], m[u], state_sem.at[1, u]),
-                pltpu.make_async_copy(v_in[u], v[u], state_sem.at[2, u]),
-            )
+    state = {}
+    for u in order:
+        state[u] = (
+            pltpu.make_async_copy(w[u].at[:, me], w_own[u], state_sem.at[0, u]),
+            pltpu.make_async_copy(m_in[u], m[u], state_sem.at[1, u]),
+            pltpu.make_async_copy(v_in[u], v[u], state_sem.at[2, u]),
         )
         for copy in state[u]:
             copy.start()
@@ -144,10 +145,10 @@
     @pl.loop(1, last)
     def _(k):
         slot = lax.rem(k, 2)
-        for u in range(units):
+        for u in order:
             load_own(k + 1, u)
             push_all(k + 1, u)
-        for u in range(units):
+        for u in order:
             terms_here(k, u)
             for d in ways:
                 block = owner(d, k) * CORES + core
@@ -161,7 +162,7 @@
                 sent(d, u)
                 send(block, d, k, u)
 
-    for u in range(units):
+    for u in order:
         terms_here(last, u)
         for copy in state[u]:
             copy.wait()
@@ -181,7 +182,7 @@
 
     @pl.loop(1, last - 1)
     def _(j):
-        for u in range(units):
+        for u in order:
             for d in ways:
                 block = behind(d, j) * CORES + core
                 arrived(block, d, last + j - 1, u)
@@ -189,35 +190,35 @@
                 send(block, d, last + j, u)
                 pass_on(block, d, u)
 
-    for u in range(units):
+    for u in order:
         for d in ways:
             block = behind(d, last - 1) * CORES + core
             arrived(block, d, 2 * last - 2, u)
-            sent(d, u)
-            if u == final:
+            if u in late:
+
+                @pl.loop(0, rows_of[u])
+                def _(row):
+                    after[d][late.index(u), row] = out[u][d, block, row]
+
+            else:
+                sent(d, u)
                 for p, (at, count) in enumerate(cuts(rows_of[u])[::-1]):
                     send(block, d, 2 * last - 1, u, pl.ds(at, count), tail_recv.at[d, p])
-            else:
-                send(block, d, 2 * last - 1, u)
             pass_on(block, d, u)
 
-    for u in range(final):
+    for p, (at, count) in enumerate(cuts(rows_of[lead])[::-1]):
         for d in ways:
             block = behind(d, last) * CORES + core
-            arrived(block, d, 2 * last - 1, u)
-            pass_on(block, d, u)
-    for p, (at, count) in enumerate(cuts(rows_of[final])[::-1]):
-        for d in ways:
-            block = behind(d, last) * CORES + core
-            wait_bytes(out[final].at[d, block, pl.ds(at, count)], tail_recv.at[d, p])
-            pass_on(block, d, final, pl.ds(at, count))
-
-    for u in range(units):
+            wait_bytes(out[lead].at[d, block, pl.ds(at, count)], tail_recv.at[d, p])
+            pass_on(block, d, lead, pl.ds(at, count))
+
+    for u in order:
         for d in ways:
             sent(d, u)
             wait_bytes(part[u].at[d], push_send.at[d, u])
-            wait_bytes(out[u].at[d, pl.ds(0, ring)], pass_send.at[d, u])
-            wait_bytes(out[u].at[d, pl.ds(0, ring)], pass_recv.at[d, u])
+            passed = out[u].at[d, pl.ds(0, last if u in late else ring)]
+            wait_bytes(passed, pass_send.at[d, u])
+            wait_bytes(passed, pass_recv.at[d, u])
 
 
 def place(*refs):
@@ -229,12 +230,30 @@
         copy.wait()
 
 
+def put(n, late, *refs):
+    blocks, out, sem = refs[len(late) : len(late) + 4], refs[len(late) + 4 : 2 * len(late) + 4], refs[-1]
+    me = lax.axis_index("dp")
+    z, core = me // CORES, me % CORES
+    ring = n // CORES
+    copies = []
+    for d in range(2):
+        block = lax.rem(z + (ring - 1 if d else 1), ring) * CORES
+        for i in range(len(late)):
+            for which, index in ((0, block + core), (2, block + 1 - core)):
+                copies.append(pltpu.make_async_copy(blocks[which + d].at[i], out[i].at[d, index], sem.at[len(copies)]))
+    for copy in copies:
+        copy.start()
+    for copy in copies:
+        copy.wait()
+
+
 def solution(mesh):
     n = mesh.shape["dp"]
 
     def step(*arrays):
         terms, weights, m, v = (arrays[i : i + 3] for i in (0, 3, 6, 9))
         units = len(terms)
+        order, late = (2, 0, 1), (0, 1)
         layers = weights[0].shape[0]
 
         def blocks(x, count):
@@ -248,10 +267,13 @@
         block = [x.shape[1:] for x in m_in]
         dma = lambda *shape: pltpu.SemaphoreType.DMA(shape)
         new = pl.pallas_call(
-            functools.partial(kernel, n, units),
-            out_shape=[pltpu.VMEM(x.shape, x.dtype) for x in (*weights_in, *m_in, *v_in)],
+            functools.partial(kernel, n, order, late),
+            out_shape=[
+                *(pltpu.VMEM(x.shape, x.dtype) for x in (*weights_in, *m_in, *v_in)),
+                *[pltpu.VMEM((len(late), *block[late[0]]), jnp.bfloat16)] * 2,
+            ],
             in_specs=[pl.BlockSpec(memory_space=pltpu.HBM)] * (4 * units),
-            out_specs=[pl.BlockSpec(memory_space=pltpu.VMEM)] * (3 * units),
+            out_specs=[pl.BlockSpec(memory_space=pltpu.VMEM)] * (3 * units + 2),
             scratch_shapes=[
                 *(pltpu.VMEM((2, 2, *b), jnp.bfloat16) for b in block),
                 *(pltpu.VMEM((2, ring, *b), jnp.bfloat16) for b in block),
@@ -270,6 +292,8 @@
             compiler_params=pltpu.CompilerParams(collective_id=0, has_side_effects=True, vmem_limit_bytes=VMEM_LIMIT),
             name="step_end",
         )(*(pltpu.with_memory_space_constraint(x, pltpu.HBM) for x in (*terms, *weights_in, *m_in, *v_in)))
+        new, after = new[: 3 * units], new[3 * units :]
+        far = [lax.ppermute(x, "dp", [(i, (i + way * CORES) % n) for i in range(n)]) for x, way in zip(after, (1, -1), strict=True)]
         new = pl.pallas_call(
             place,
             out_shape=[jax.ShapeDtypeStruct(x.shape, x.dtype) for x in new],
@@ -278,7 +302,23 @@
             scratch_shapes=[dma(len(new))],
             compiler_params=pltpu.CompilerParams(vmem_limit_bytes=VMEM_LIMIT),
             name="place",
+            cost_estimate=pl.CostEstimate(flops=3 * 10**9, bytes_accessed=4 * 10**7, transcendentals=0),
         )(*(pltpu.with_memory_space_constraint(x, pltpu.VMEM) for x in new))
+        new = list(new)
+        *far, new[late[0]] = lax.optimization_barrier((*far, new[late[0]]))
+        near = [lax.ppermute(x, "dp", [(i, i ^ 1) for i in range(n)]) for x in far]
+        done = pl.pallas_call(
+            functools.partial(put, n, late),
+            out_shape=[jax.ShapeDtypeStruct(new[u].shape, new[u].dtype) for u in late],
+            in_specs=[pl.BlockSpec(memory_space=pltpu.HBM)] * len(late) + [pl.BlockSpec(memory_space=pltpu.VMEM)] * 4,
+            out_specs=[pl.BlockSpec(memory_space=pltpu.HBM)] * len(late),
+            scratch_shapes=[dma(4 * len(late))],
+            input_output_aliases={i: i for i in range(len(late))},
+            compiler_params=pltpu.CompilerParams(vmem_limit_bytes=VMEM_LIMIT),
+            name="put",
+        )(*(new[u] for u in late), *(pltpu.with_memory_space_constraint(x, pltpu.VMEM) for x in (*far, *near)))
+        for u, x in zip(late, done, strict=True):
+            new[u] = x
         return tuple(x.reshape(like.shape) for x, like in zip(new, (*weights, *m, *v), strict=True))
 
     all_of, cut = P(None, None, None), P(None, "dp", None)

time: 283 us -> 280 us (0.989)
  Pallas kernels: 283 us -> 272 us
  waiting for transfers between devices: 0 us -> 3.99 us
  starting transfers between devices: 0 us -> 3.79 us
    pallas_call x1 -> x2, Pallas kernels: 271 us -> 260 us  [the longest x1 259 us: step(): pl.pallas_call(functools.partial(kernel, n, order, late), out_shape=[*(pl...]
    ppermute x0 -> x4, waiting for transfers between devices: none -> 3.99 us  [the longest x2 2.42 us: step(): near = [lax.ppermute(x, 'dp', [(i, i ^ 1) for i in range(n)]) for x in far]]
    ppermute x0 -> x4, starting transfers between devices: none -> 3.79 us  [the longest x2 2.77 us: step(): lax.ppermute(x, 'dp', [(i, (i + way * CORES) % n) for i in range(n)])]
  transfers between devices with their start and end apart: 0 -> 4, of which waited for: 0 -> 3; matrix products, arithmetic and copies ran while one was open for 0% -> 0% of each run, Pallas kernels for 0% -> 4%
where the time goes in v3:
time: 280 us
  Pallas kernels  272 us (97%)
  waiting for transfers between devices  3.99 us (1%)
  starting transfers between devices  3.79 us (1%)
    pallas_call x1, Pallas kernels, step(): pl.pallas_call(functools.partial(kernel, n, order, late), out_shape=[*(pl...  259 us
    pallas_call x1, Pallas kernels, step(): pl.pallas_call(place, out_shape=[jax.ShapeDtypeStruct(x.shape, x.dtype) f...  11.3 us
  transfers between devices with their start and end apart: 4, of which 3 were waited for; matrix products, arithmetic and copies ran while one was open for 0% of the time, Pallas kernels for 4%

profile of v3, /device:TPU:21, one launch (start us, length us, event | category | flops | bytes accessed | tf_op | source)
XLA Modules:
  0.0 280.1 jit_solution(15860405105098578976)
XLA Ops:
  0.6 258.9 %step_end.1 = (bf16[2,16,7,8,2560]{4,3,2,1,0:T(8,128)(2,1)S(1)}, bf16[2,16,7,8,2560]{4,3,2,1,0:T(8,128)(2,1)S(1)}, bf16[2,16,20,8,896]{4,3,2,1,0:T(8,128)(2,1)S(...) custom-call(bf16[2,16,7,8,2560]{4,3,2,1,0:T(8,128)(2,1)} %bitcast.23, ...), custom_call_target="tpu_custom_call" | custom-call | tf_op jit(solution)/shard_map/step_end/pallas_call | solution.py:269
  259.5 0.8 collective-permute-start
  260.3 2.0 collective-permute-start.1
  262.3 11.3 %place.1 = (bf16[2,16,7,8,2560]{4,3,2,1,0:T(8,128)(2,1)}, bf16[2,16,7,8,2560]{4,3,2,1,0:T(8,128)(2,1)}, bf16[2,16,20,8,896]{4,3,2,1,0:T(8,128)(2,1)}, f32[2,7,8,...) custom-call(bf16[2,16,7,8,2560]{4,3,2,1,0:T(8,128)(2,1)S(1)} %get-tu, ...), custom_call_target="tpu_custom_call" | custom-call | flops 3000000000 | bytes 40000000 | tf_op jit(solution)/shard_map/place/pallas_call | solution.py:297
  273.7 1.6 collective-permute-done.refs_2_
  275.2 0.0 collective-permute-done.1.refs_3_
  275.2 1.0 collective-permute-start.2
  276.2 0.0 collective-permute-start.3
  276.2 1.6 collective-permute-done.2.refs_4_
  277.8 0.8 collective-permute-done.3.refs_5_
  278.7 1.4 put.1
Async XLA Ops:
  259.5 15.7 %collective-permute-start = (bf16[2,7,8,2560]{3,2,1,0:T(8,128)(2,1)S(1)}, bf16[2,7,8,2560]{3,2,1,0:T(8,128)(2,1)S(1)}, u32[]{:S(2)}, u32[]{:S(2)}) collective-permute-start(bf16[2,7,8,2560]{3,2,1,0:T(8,128)(2,1)S(1)} %get-tuple-element.34), channel_id=1, source_target_pairs={{0,2},{1,3},{2,4},{3,5},{4,6},{5,7},{6,8},{7,9},{8,10},{9,11},{10,... | collective-permute-start | bytes 1720328 | tf_op jit(solution)/shard_map/ppermute | solution.py:296
  260.3 14.9 %collective-permute-start.1 = (bf16[2,7,8,2560]{3,2,1,0:T(8,128)(2,1)S(1)}, bf16[2,7,8,2560]{3,2,1,0:T(8,128)(2,1)S(1)}, u32[]{:S(2)}, u32[]{:S(2)}) collective-permute-start(bf16[2,7,8,2560]{3,2,1,0:T(8,128)(2,1)S(1)} %get-tuple-element.35), channel_id=1, source_target_pairs={{0,14},{1,15},{2,0},{3,1},{4,2},{5,3},{6,4},{7,5},{8,6},{9,7},{10,... | collective-permute-start | bytes 1720328 | tf_op jit(solution)/shard_map/ppermute | solution.py:296
  275.2 2.6 collective-permute-start.2
  276.2 2.4 collective-permute-start.3

commit v4 on v3

--- a/solution.py
+++ b/solution.py
@@ -30,7 +30,7 @@
     g, w, m_in, v_in, out, m, v = (refs[i * units : (i + 1) * units] for i in range(7))
     after, refs = refs[7 * units : 7 * units + 2], refs[7 * units + 2 :]
     own, part, w_own = (refs[i * units : (i + 1) * units] for i in range(3))
-    own_sem, state_sem, push_send, push_recv, ring_send, ring_recv, pass_send, pass_recv, first_recv, tail_recv = refs[3 * units :]
+    own_sem, state_sem, push_send, push_recv, ring_send, ring_recv, pass_send, pass_recv, first_recv = refs[3 * units :]
 
     me = lax.axis_index("dp")
     z, core = me // CORES, me % CORES
@@ -39,6 +39,7 @@
     last = ring - 1
     ways = (0, 1)
     lead, *others = order
+    tail = order[-1]
 
     def chip(offset):
         return lax.rem(z + offset + 2 * ring, ring)
@@ -180,43 +181,45 @@
             send(me, d, last, u)
             pass_on(me, d, u)
 
-    @pl.loop(1, last - 1)
+    def forward(d, j, u):
+        block = behind(d, j) * CORES + core
+        arrived(block, d, last + j - 1, u)
+        sent(d, u)
+        send(block, d, last + j, u)
+        pass_on(block, d, u)
+
+    @pl.loop(1, last - 2)
     def _(j):
         for u in order:
             for d in ways:
-                block = behind(d, j) * CORES + core
-                arrived(block, d, last + j - 1, u)
-                sent(d, u)
-                send(block, d, last + j, u)
-                pass_on(block, d, u)
-
-    for u in order:
+                forward(d, j, u)
+
+    for u in order:
+        if u == tail:
+            for d in ways:
+                forward(d, last - 1, lead)
+        for d in ways:
+            forward(d, last - 2, u)
+
+    for u in others:
+        if u == tail:
+            for d in ways:
+                block = behind(d, last) * CORES + core
+                arrived(block, d, 2 * last - 1, lead)
+                pass_on(block, d, lead)
         for d in ways:
             block = behind(d, last - 1) * CORES + core
             arrived(block, d, 2 * last - 2, u)
-            if u in late:
-
-                @pl.loop(0, rows_of[u])
-                def _(row):
-                    after[d][late.index(u), row] = out[u][d, block, row]
-
-            else:
-                sent(d, u)
-                for p, (at, count) in enumerate(cuts(rows_of[u])[::-1]):
-                    send(block, d, 2 * last - 1, u, pl.ds(at, count), tail_recv.at[d, p])
-            pass_on(block, d, u)
-
-    for p, (at, count) in enumerate(cuts(rows_of[lead])[::-1]):
-        for d in ways:
-            block = behind(d, last) * CORES + core
-            wait_bytes(out[lead].at[d, block, pl.ds(at, count)], tail_recv.at[d, p])
-            pass_on(block, d, lead, pl.ds(at, count))
+
+            @pl.loop(0, rows_of[u])
+            def _(row):
+                after[d][late.index(u), row] = out[u][d, block, row]
 
     for u in order:
         for d in ways:
             sent(d, u)
             wait_bytes(part[u].at[d], push_send.at[d, u])
-            passed = out[u].at[d, pl.ds(0, last if u in late else ring)]
+            passed = out[u].at[d, pl.ds(0, last - 1 if u in late else ring)]
             wait_bytes(passed, pass_send.at[d, u])
             wait_bytes(passed, pass_recv.at[d, u])
 
@@ -230,17 +233,16 @@
         copy.wait()
 
 
-def put(n, late, *refs):
-    blocks, out, sem = refs[len(late) : len(late) + 4], refs[len(late) + 4 : 2 * len(late) + 4], refs[-1]
+def put(n, late, where, *refs):
+    count = len(late)
+    blocks, out, sem = refs[count : count + len(where)], refs[count + len(where) : -1], refs[-1]
     me = lax.axis_index("dp")
     z, core = me // CORES, me % CORES
     ring = n // CORES
     copies = []
-    for d in range(2):
-        block = lax.rem(z + (ring - 1 if d else 1), ring) * CORES
-        for i in range(len(late)):
-            for which, index in ((0, block + core), (2, block + 1 - core)):
-                copies.append(pltpu.make_async_copy(blocks[which + d].at[i], out[i].at[d, index], sem.at[len(copies)]))
+    for part, (d, back, partners) in zip(blocks, where, strict=True):
+        index = lax.rem(z + (back if d else ring - back), ring) * CORES + (1 - core if partners else core)
+        copies += [pltpu.make_async_copy(part.at[i], out[i].at[d, index], sem.at[len(copies) + i]) for i in range(count)]
     for copy in copies:
         copy.start()
     for copy in copies:
@@ -287,13 +289,14 @@
                 dma(2, units),
                 dma(2, units),
                 dma(2, 3),
-                dma(2, 3),
             ],
             compiler_params=pltpu.CompilerParams(collective_id=0, has_side_effects=True, vmem_limit_bytes=VMEM_LIMIT),
             name="step_end",
         )(*(pltpu.with_memory_space_constraint(x, pltpu.HBM) for x in (*terms, *weights_in, *m_in, *v_in)))
         new, after = new[: 3 * units], new[3 * units :]
+        across = [(i, i ^ 1) for i in range(n)]
         far = [lax.ppermute(x, "dp", [(i, (i + way * CORES) % n) for i in range(n)]) for x, way in zip(after, (1, -1), strict=True)]
+        near = [lax.ppermute(x, "dp", across) for x in after]
         new = pl.pallas_call(
             place,
             out_shape=[jax.ShapeDtypeStruct(x.shape, x.dtype) for x in new],
@@ -306,19 +309,24 @@
         )(*(pltpu.with_memory_space_constraint(x, pltpu.VMEM) for x in new))
         new = list(new)
         *far, new[late[0]] = lax.optimization_barrier((*far, new[late[0]]))
-        near = [lax.ppermute(x, "dp", [(i, i ^ 1) for i in range(n)]) for x in far]
-        done = pl.pallas_call(
-            functools.partial(put, n, late),
-            out_shape=[jax.ShapeDtypeStruct(new[u].shape, new[u].dtype) for u in late],
-            in_specs=[pl.BlockSpec(memory_space=pltpu.HBM)] * len(late) + [pl.BlockSpec(memory_space=pltpu.VMEM)] * 4,
-            out_specs=[pl.BlockSpec(memory_space=pltpu.HBM)] * len(late),
-            scratch_shapes=[dma(4 * len(late))],
-            input_output_aliases={i: i for i in range(len(late))},
-            compiler_params=pltpu.CompilerParams(vmem_limit_bytes=VMEM_LIMIT),
-            name="put",
-        )(*(new[u] for u in late), *(pltpu.with_memory_space_constraint(x, pltpu.VMEM) for x in (*far, *near)))
-        for u, x in zip(late, done, strict=True):
-            new[u] = x
+        last = n // CORES - 1
+        for parts, where in (
+            ((*far, *near), ((0, last, 0), (1, last, 0), (0, last - 1, 1), (1, last - 1, 1))),
+            ([lax.ppermute(x, "dp", across) for x in far], ((0, last, 1), (1, last, 1))),
+        ):
+            done = pl.pallas_call(
+                functools.partial(put, n, late, where),
+                out_shape=[jax.ShapeDtypeStruct(new[u].shape, new[u].dtype) for u in late],
+                in_specs=[pl.BlockSpec(memory_space=pltpu.HBM)] * len(late) + [pl.BlockSpec(memory_space=pltpu.VMEM)] * len(parts),
+                out_specs=[pl.BlockSpec(memory_space=pltpu.HBM)] * len(late),
+                scratch_shapes=[dma(len(where) * len(late))],
+                input_output_aliases={i: i for i in range(len(late))},
+                compiler_params=pltpu.CompilerParams(vmem_limit_bytes=VMEM_LIMIT),
+                cost_estimate=pl.CostEstimate(flops=2 * 10**8, bytes_accessed=2 * 10**6, transcendentals=0),
+                name="put",
+            )(*(new[u] for u in late), *(pltpu.with_memory_space_constraint(x, pltpu.VMEM) for x in parts))
+            for u, x in zip(late, done, strict=True):
+                new[u] = x
         return tuple(x.reshape(like.shape) for x, like in zip(new, (*weights, *m, *v), strict=True))
 
     all_of, cut = P(None, None, None), P(None, "dp", None)

time: 280 us -> 279 us (level)
  transfers between devices with their start and end apart: 4 -> 6, of which waited for: 3 -> 3; matrix products, arithmetic and copies ran while one was open for 0% -> 0% of each run, Pallas kernels for 4% -> 5%
where the time goes in v4:
time: 279 us
  Pallas kernels  272 us (97%)
  starting transfers between devices  4.98 us (2%)
    pallas_call x1, Pallas kernels, step(): pl.pallas_call(functools.partial(kernel, n, order, late), out_shape=[*(pl...  258 us
    pallas_call x1, Pallas kernels, step(): pl.pallas_call(place, out_shape=[jax.ShapeDtypeStruct(x.shape, x.dtype) f...  11.3 us
  transfers between devices with their start and end apart: 6, of which 3 were waited for; matrix products, arithmetic and copies ran while one was open for 0% of the time, Pallas kernels for 5%

profile of v4, /device:TPU:21, one launch (start us, length us, event | category | flops | bytes accessed | tf_op | source)
XLA Modules:
  0.0 278.6 jit_solution(14536042635670497665)
XLA Ops:
  0.6 257.8 %step_end.1 = (bf16[2,16,7,8,2560]{4,3,2,1,0:T(8,128)(2,1)S(1)}, bf16[2,16,7,8,2560]{4,3,2,1,0:T(8,128)(2,1)S(1)}, bf16[2,16,20,8,896]{4,3,2,1,0:T(8,128)(2,1)S(...) custom-call(bf16[2,16,7,8,2560]{4,3,2,1,0:T(8,128)(2,1)} %bitcast.23, ...), custom_call_target="tpu_custom_call" | custom-call | tf_op jit(solution)/shard_map/step_end/pallas_call | solution.py:271
  258.5 0.8 collective-permute-start
  259.3 2.0 collective-permute-start.1
  261.2 1.0 collective-permute-start.2
  262.2 0.0 collective-permute-start.3
  262.2 11.3 %place.1 = (bf16[2,16,7,8,2560]{4,3,2,1,0:T(8,128)(2,1)}, bf16[2,16,7,8,2560]{4,3,2,1,0:T(8,128)(2,1)}, bf16[2,16,20,8,896]{4,3,2,1,0:T(8,128)(2,1)}, f32[2,7,8,...) custom-call(bf16[2,16,7,8,2560]{4,3,2,1,0:T(8,128)(2,1)S(1)} %get-tu, ...), custom_call_target="tpu_custom_call" | custom-call | flops 3000000000 | bytes 40000000 | tf_op jit(solution)/shard_map/place/pallas_call | solution.py:300
  273.5 0.4 collective-permute-done.refs_2_
  273.9 0.0 collective-permute-done.1.refs_3_
  273.9 1.3 collective-permute-start.4
  275.2 0.0 collective-permute-start.5
  275.2 0.0 collective-permute-done.2.refs_4_
  275.2 0.0 collective-permute-done.3.refs_5_
  275.2 1.5 put.2
  276.6 0.1 collective-permute-done.4.refs_2_
  276.8 0.8 collective-permute-done.5.refs_3_
  277.6 1.0 put.3
Async XLA Ops:
  258.5 15.4 %collective-permute-start = (bf16[2,7,8,2560]{3,2,1,0:T(8,128)(2,1)S(1)}, bf16[2,7,8,2560]{3,2,1,0:T(8,128)(2,1)S(1)}, u32[]{:S(2)}, u32[]{:S(2)}) collective-permute-start(bf16[2,7,8,2560]{3,2,1,0:T(8,128)(2,1)S(1)} %get-tuple-element.36), channel_id=1, source_target_pairs={{0,2},{1,3},{2,4},{3,5},{4,6},{5,7},{6,8},{7,9},{8,10},{9,11},{10,... | collective-permute-start | bytes 1720328 | tf_op jit(solution)/shard_map/ppermute | solution.py:298
  259.3 14.7 %collective-permute-start.1 = (bf16[2,7,8,2560]{3,2,1,0:T(8,128)(2,1)S(1)}, bf16[2,7,8,2560]{3,2,1,0:T(8,128)(2,1)S(1)}, u32[]{:S(2)}, u32[]{:S(2)}) collective-permute-start(bf16[2,7,8,2560]{3,2,1,0:T(8,128)(2,1)S(1)} %get-tuple-element.37), channel_id=1, source_target_pairs={{0,14},{1,15},{2,0},{3,1},{4,2},{5,3},{6,4},{7,5},{8,6},{9,7},{10,... | collective-permute-start | bytes 1720328 | tf_op jit(solution)/shard_map/ppermute | solution.py:298
  261.2 13.9 %collective-permute-start.2 = (bf16[2,7,8,2560]{3,2,1,0:T(8,128)(2,1)S(1)}, bf16[2,7,8,2560]{3,2,1,0:T(8,128)(2,1)S(1)}, u32[]{:S(2)}, u32[]{:S(2)}) collective-permute-start(bf16[2,7,8,2560]{3,2,1,0:T(8,128)(2,1)S(1)} %get-tuple-element.36), channel_id=1, source_target_pairs={{0,1},{1,0},{2,3},{3,2},{4,5},{5,4},{6,7},{7,6},{8,9},{9,8},{10,11... | collective-permute-start | bytes 1720328 | tf_op jit(solution)/shard_map/ppermute | solution.py:299
  262.2 13.0 %collective-permute-start.3 = (bf16[2,7,8,2560]{3,2,1,0:T(8,128)(2,1)S(1)}, bf16[2,7,8,2560]{3,2,1,0:T(8,128)(2,1)S(1)}, u32[]{:S(2)}, u32[]{:S(2)}) collective-permute-start(bf16[2,7,8,2560]{3,2,1,0:T(8,128)(2,1)S(1)} %get-tuple-element.37), channel_id=1, source_target_pairs={{0,1},{1,0},{2,3},{3,2},{4,5},{5,4},{6,7},{7,6},{8,9},{9,8},{10,11... | collective-permute-start | bytes 1720328 | tf_op jit(solution)/shard_map/ppermute | solution.py:299
  273.9 2.9 %collective-permute-start.4 = (bf16[2,7,8,2560]{3,2,1,0:T(8,128)(2,1)S(1)}, bf16[2,7,8,2560]{3,2,1,0:T(8,128)(2,1)S(1)}, u32[]{:S(2)}, u32[]{:S(2)}) collective-permute-start(bf16[2,7,8,2560]{3,2,1,0:T(8,128)(2,1)S(1)} %collective-permute-done.refs_2_), channel_id=1, source_target_pairs={{0,1},{1,0},{2,3},{3,2},{4,5},{5,4},{6,7},{7,6},{8,9},{9,8},{10,11... | collective-permute-start | bytes 1720328 | tf_op jit(solution)/shard_map/ppermute | solution.py:315
  275.2 2.4 collective-permute-start.5

commit v5 on v4

--- a/solution.py
+++ b/solution.py
@@ -7,6 +7,7 @@
 from jax.experimental.pallas import tpu as pltpu
 from jax.sharding import PartitionSpec as P
 
+
 CORES = 2
 SUBLANES = 8
 VMEM_LIMIT = 20 * 2**20
@@ -30,7 +31,7 @@
     g, w, m_in, v_in, out, m, v = (refs[i * units : (i + 1) * units] for i in range(7))
     after, refs = refs[7 * units : 7 * units + 2], refs[7 * units + 2 :]
     own, part, w_own = (refs[i * units : (i + 1) * units] for i in range(3))
-    own_sem, state_sem, push_send, push_recv, ring_send, ring_recv, pass_send, pass_recv, first_recv = refs[3 * units :]
+    own_sem, state_sem, across_send, push_recv, ring_send, ring_recv, pass_recv, first_recv = refs[3 * units :]
 
     me = lax.axis_index("dp")
     z, core = me // CORES, me % CORES
@@ -66,7 +67,7 @@
 
     def push(d, k, u, sem, rows=slice(None)):
         pltpu.make_async_remote_copy(
-            g[u].at[d, owner(d, k) * CORES + 1 - core, rows], part[u].at[d, k, rows], push_send.at[d, u], sem, **to(partner)
+            g[u].at[d, owner(d, k) * CORES + 1 - core, rows], part[u].at[d, k, rows], across_send.at[u], sem, **to(partner)
         ).start()
 
     def push_all(k, u):
@@ -80,17 +81,17 @@
     def send(block, d, t, u, rows=slice(None), sem=None):
         piece = out[u].at[d, block, rows]
         sem = ring_recv.at[lax.rem(t, 3), d, u] if sem is None else sem
-        pltpu.make_async_remote_copy(piece, piece, ring_send.at[d, u], sem, **following(d)).start()
-
-    def sent(d, u):
-        wait_bytes(out[u].at[d, 0], ring_send.at[d, u])
+        pltpu.make_async_remote_copy(piece, piece, ring_send.at[u], sem, **following(d)).start()
+
+    def sent(u):
+        wait_bytes(out[u].at[:, 0], ring_send.at[u])
 
     def arrived(block, d, t, u):
         wait_bytes(out[u].at[d, block], ring_recv.at[lax.rem(t, 3), d, u])
 
     def pass_on(block, d, u, rows=slice(None)):
         piece = out[u].at[d, block, rows]
-        pltpu.make_async_remote_copy(piece, piece, pass_send.at[d, u], pass_recv.at[d, u], **to(partner)).start()
+        pltpu.make_async_remote_copy(piece, piece, across_send.at[u], pass_recv.at[u], **to(partner)).start()
 
     def terms(slot, d, k, u, row):
         return own[u][slot, d, row].astype(jnp.float32) + part[u][d, k, row].astype(jnp.float32)
@@ -160,7 +161,8 @@
                     total = out[u][d, block, row].astype(jnp.float32) + terms(slot, d, k, u, row)
                     out[u][d, block, row] = total.astype(out[u].dtype)
 
-                sent(d, u)
+                if d == 0:
+                    sent(u)
                 send(block, d, k, u)
 
     for u in order:
@@ -177,14 +179,16 @@
                 new = adamw(w_own[u][d, row].astype(jnp.float32), m[u][d, row], v[u][d, row], gradient)
                 out[u][d, me, row], m[u][d, row], v[u][d, row] = new
 
-            sent(d, u)
+            if d == 0:
+                sent(u)
             send(me, d, last, u)
             pass_on(me, d, u)
 
     def forward(d, j, u):
         block = behind(d, j) * CORES + core
         arrived(block, d, last + j - 1, u)
-        sent(d, u)
+        if d == 0:
+            sent(u)
         send(block, d, last + j, u)
         pass_on(block, d, u)
 
@@ -216,12 +220,10 @@
                 after[d][late.index(u), row] = out[u][d, block, row]
 
     for u in order:
-        for d in ways:
-            sent(d, u)
-            wait_bytes(part[u].at[d], push_send.at[d, u])
-            passed = out[u].at[d, pl.ds(0, last - 1 if u in late else ring)]
-            wait_bytes(passed, pass_send.at[d, u])
-            wait_bytes(passed, pass_recv.at[d, u])
+        sent(u)
+        passed = last - 1 if u in late else ring
+        wait_bytes(out[u].at[:, pl.ds(0, ring + passed)], across_send.at[u])
+        wait_bytes(out[u].at[:, pl.ds(0, passed)], pass_recv.at[u])
 
 
 def place(*refs):
@@ -235,7 +237,7 @@
 
 def put(n, late, where, *refs):
     count = len(late)
-    blocks, out, sem = refs[count : count + len(where)], refs[count + len(where) : -1], refs[-1]
+    blocks, out, sem = refs[count : count + len(where)], refs[-1 - count : -1], refs[-1]
     me = lax.axis_index("dp")
     z, core = me // CORES, me % CORES
     ring = n // CORES
@@ -249,10 +251,17 @@
         copy.wait()
 
 
+def marker(ref, out):
+    out[...] = jnp.zeros_like(out)
+
+
 def solution(mesh):
     n = mesh.shape["dp"]
 
     def step(*arrays):
+        return whole_step(*arrays)
+
+    def whole_step(*arrays):
         terms, weights, m, v = (arrays[i : i + 3] for i in (0, 3, 6, 9))
         units = len(terms)
         order, late = (2, 0, 1), (0, 1)
@@ -282,12 +291,11 @@
                 *(pltpu.VMEM((2, *b), jnp.bfloat16) for b in block),
                 dma(2, units),
                 dma(3, units),
-                dma(2, units),
+                dma(units),
                 dma(ring, units),
-                dma(2, units),
+                dma(units),
                 dma(3, 2, units),
-                dma(2, units),
-                dma(2, units),
+                dma(units),
                 dma(2, 3),
             ],
             compiler_params=pltpu.CompilerParams(collective_id=0, has_side_effects=True, vmem_limit_bytes=VMEM_LIMIT),
@@ -295,9 +303,11 @@
         )(*(pltpu.with_memory_space_constraint(x, pltpu.HBM) for x in (*terms, *weights_in, *m_in, *v_in)))
         new, after = new[: 3 * units], new[3 * units :]
         across = [(i, i ^ 1) for i in range(n)]
-        far = [lax.ppermute(x, "dp", [(i, (i + way * CORES) % n) for i in range(n)]) for x, way in zip(after, (1, -1), strict=True)]
+        far = []
+        for d, way in enumerate((1, -1)):
+            far.append(lax.ppermute(after[d], "dp", [(i, (i + way * CORES) % n) for i in range(n)]))
         near = [lax.ppermute(x, "dp", across) for x in after]
-        new = pl.pallas_call(
+        writer = pl.pallas_call(
             place,
             out_shape=[jax.ShapeDtypeStruct(x.shape, x.dtype) for x in new],
             in_specs=[pl.BlockSpec(memory_space=pltpu.VMEM)] * len(new),
@@ -306,14 +316,11 @@
             compiler_params=pltpu.CompilerParams(vmem_limit_bytes=VMEM_LIMIT),
             name="place",
             cost_estimate=pl.CostEstimate(flops=3 * 10**9, bytes_accessed=4 * 10**7, transcendentals=0),
-        )(*(pltpu.with_memory_space_constraint(x, pltpu.VMEM) for x in new))
-        new = list(new)
-        *far, new[late[0]] = lax.optimization_barrier((*far, new[late[0]]))
+        )
+        new = list(writer(*(pltpu.with_memory_space_constraint(x, pltpu.VMEM) for x in new)))
         last = n // CORES - 1
-        for parts, where in (
-            ((*far, *near), ((0, last, 0), (1, last, 0), (0, last - 1, 1), (1, last - 1, 1))),
-            ([lax.ppermute(x, "dp", across) for x in far], ((0, last, 1), (1, last, 1))),
-        ):
+
+        def write(parts, where):
             done = pl.pallas_call(
                 functools.partial(put, n, late, where),
                 out_shape=[jax.ShapeDtypeStruct(new[u].shape, new[u].dtype) for u in late],
@@ -327,13 +334,33 @@
             )(*(new[u] for u in late), *(pltpu.with_memory_space_constraint(x, pltpu.VMEM) for x in parts))
             for u, x in zip(late, done, strict=True):
                 new[u] = x
+
+        def swap(d):
+            far[d], new[late[0]] = lax.optimization_barrier((far[d], new[late[0]]))
+            return lax.ppermute(far[d], "dp", across)
+
+        swapped = {1: swap(1)}
+        mark = pl.pallas_call(
+            marker,
+            out_shape=pltpu.VMEM((SUBLANES, 128), jnp.float32),
+            in_specs=[pl.BlockSpec(memory_space=pltpu.VMEM)],
+            out_specs=pl.BlockSpec(memory_space=pltpu.VMEM),
+            compiler_params=pltpu.CompilerParams(vmem_limit_bytes=VMEM_LIMIT),
+            cost_estimate=pl.CostEstimate(flops=10**5, bytes_accessed=10**4, transcendentals=0),
+            name="mark",
+        )(far[1])
+        far[0], mark = lax.optimization_barrier((far[0], mark))
+        swapped[0] = swap(0)
+        write((*far, *near, mark), ((0, last, 0), (1, last, 0), (0, last - 1, 1), (1, last - 1, 1)))
+        write((swapped[0], swapped[1]), ((0, last, 1), (1, last, 1)))
         return tuple(x.reshape(like.shape) for x, like in zip(new, (*weights, *m, *v), strict=True))
 
     all_of, cut = P(None, None, None), P(None, "dp", None)
-    return jax.shard_map(
+    step = jax.shard_map(
         step,
         mesh=mesh,
         in_specs=(P(("rep", "dp"), None, None, None),) * 3 + (all_of,) * 3 + (cut,) * 6,
         out_specs=(P("rep", None, None),) * 3 + (P("rep", "dp", None),) * 6,
         check_vma=False,
     )
+    return step

time: 279 us -> 281 us (level)
    pallas_call x4 -> x5, Pallas kernels: 272 us -> 272 us  [the longest x1 258 us: whole_step(): pl.pallas_call(functools.partial(kernel, n, order, late), out_shape=[*(pl...]
  transfers between devices with their start and end apart: 6 -> 6, of which waited for: 3 -> 4; matrix products, arithmetic and copies ran while one was open for 0% -> 0% of each run, Pallas kernels for 5% -> 5%
where the time goes in v5:
time: 281 us
  Pallas kernels  272 us (97%)
  starting transfers between devices  4.2 us (1%)
  waiting for transfers between devices  3.99 us (1%)
    pallas_call x1, Pallas kernels, whole_step(): pl.pallas_call(functools.partial(kernel, n, order, late), out_shape=[*(pl...  258 us
    pallas_call x1, Pallas kernels, whole_step(): writer(*(pltpu.with_memory_space_constraint(x, pltpu.VMEM) for x in new))  11.3 us
  transfers between devices with their start and end apart: 6, of which 4 were waited for; matrix products, arithmetic and copies ran while one was open for 0% of the time, Pallas kernels for 5%

profile of v5, /device:TPU:21, one launch (start us, length us, event | category | flops | bytes accessed | tf_op | source)
XLA Modules:
  0.0 280.6 jit_solution(3595283561459055400)
XLA Ops:
  0.6 257.8 %step_end.1 = (bf16[2,16,7,8,2560]{4,3,2,1,0:T(8,128)(2,1)S(1)}, bf16[2,16,7,8,2560]{4,3,2,1,0:T(8,128)(2,1)S(1)}, bf16[2,16,20,8,896]{4,3,2,1,0:T(8,128)(2,1)S(...) custom-call(bf16[2,16,7,8,2560]{4,3,2,1,0:T(8,128)(2,1)} %bitcast.23, ...), custom_call_target="tpu_custom_call" | custom-call | tf_op jit(solution)/shard_map/step_end/pallas_call | solution.py:280
  258.5 2.0 collective-permute-start.1
  260.5 0.0 collective-permute-start
  260.5 0.7 collective-permute-start.2
  261.2 0.0 collective-permute-start.3
  261.2 11.3 %place.1 = (bf16[2,16,7,8,2560]{4,3,2,1,0:T(8,128)(2,1)}, bf16[2,16,7,8,2560]{4,3,2,1,0:T(8,128)(2,1)}, bf16[2,16,20,8,896]{4,3,2,1,0:T(8,128)(2,1)}, f32[2,7,8,...) custom-call(bf16[2,16,7,8,2560]{4,3,2,1,0:T(8,128)(2,1)S(1)} %get-tu, ...), custom_call_target="tpu_custom_call" | custom-call | flops 3000000000 | bytes 40000000 | tf_op jit(solution)/shard_map/place/pallas_call | solution.py:320
  272.5 0.2 collective-permute-done.1.ref.refs_3_
  272.7 2.8 %collective-permute-done.refs_2_ = bf16[2,7,8,2560]{3,2,1,0:T(8,128)(2,1)S(1)} collective-permute-done((bf16[2,7,8,2560]{3,2,1,0:T(8,128)(2,1)S(1)}, bf16[2,7,8,2560]{3,2,1,0:T(8,128)(2,1)S(1)}, u32[]{:S(2)}, u32[]{:S(2)}) %collective-permute-start) | collective-permute-done | bytes 573472 | tf_op jit(solution)/shard_map/ppermute | solution.py:308
  275.6 1.5 collective-permute-start.4
  277.1 0.0 collective-permute-start.5
  277.1 0.0 collective-permute-done.2.refs_4_
  277.1 0.0 collective-permute-done.3.refs_5_
  277.1 1.5 put.2
  278.6 0.1 collective-permute-done.4.refs_2_
  278.7 0.8 collective-permute-done.5.refs_3_
  279.5 1.0 put.3
  (1 shorter events, 0.0 us)
Async XLA Ops:
  258.5 14.2 %collective-permute-start.1 = (bf16[2,7,8,2560]{3,2,1,0:T(8,128)(2,1)S(1)}, bf16[2,7,8,2560]{3,2,1,0:T(8,128)(2,1)S(1)}, u32[]{:S(2)}, u32[]{:S(2)}) collective-permute-start(bf16[2,7,8,2560]{3,2,1,0:T(8,128)(2,1)S(1)} %get-tuple-element.40), channel_id=1, source_target_pairs={{0,14},{1,15},{2,0},{3,1},{4,2},{5,3},{6,4},{7,5},{8,6},{9,7},{10,... | collective-permute-start | bytes 1720328 | tf_op jit(solution)/shard_map/ppermute | solution.py:308
  260.5 15.1 %collective-permute-start = (bf16[2,7,8,2560]{3,2,1,0:T(8,128)(2,1)S(1)}, bf16[2,7,8,2560]{3,2,1,0:T(8,128)(2,1)S(1)}, u32[]{:S(2)}, u32[]{:S(2)}) collective-permute-start(bf16[2,7,8,2560]{3,2,1,0:T(8,128)(2,1)S(1)} %get-tuple-element.39), channel_id=1, source_target_pairs={{0,2},{1,3},{2,4},{3,5},{4,6},{5,7},{6,8},{7,9},{8,10},{9,11},{10,... | collective-permute-start | bytes 1720328 | tf_op jit(solution)/shard_map/ppermute | solution.py:308
  260.5 16.6 %collective-permute-start.2 = (bf16[2,7,8,2560]{3,2,1,0:T(8,128)(2,1)S(1)}, bf16[2,7,8,2560]{3,2,1,0:T(8,128)(2,1)S(1)}, u32[]{:S(2)}, u32[]{:S(2)}) collective-permute-start(bf16[2,7,8,2560]{3,2,1,0:T(8,128)(2,1)S(1)} %get-tuple-element.39), channel_id=1, source_target_pairs={{0,1},{1,0},{2,3},{3,2},{4,5},{5,4},{6,7},{7,6},{8,9},{9,8},{10,11... | collective-permute-start | bytes 1720328 | tf_op jit(solution)/shard_map/ppermute | solution.py:309
  261.2 15.9 %collective-permute-start.3 = (bf16[2,7,8,2560]{3,2,1,0:T(8,128)(2,1)S(1)}, bf16[2,7,8,2560]{3,2,1,0:T(8,128)(2,1)S(1)}, u32[]{:S(2)}, u32[]{:S(2)}) collective-permute-start(bf16[2,7,8,2560]{3,2,1,0:T(8,128)(2,1)S(1)} %get-tuple-element.40), channel_id=1, source_target_pairs={{0,1},{1,0},{2,3},{3,2},{4,5},{5,4},{6,7},{7,6},{8,9},{9,8},{10,11... | collective-permute-start | bytes 1720328 | tf_op jit(solution)/shard_map/ppermute | solution.py:309
  275.6 3.1 %collective-permute-start.4 = (bf16[2,7,8,2560]{3,2,1,0:T(8,128)(2,1)S(1)}, bf16[2,7,8,2560]{3,2,1,0:T(8,128)(2,1)S(1)}, u32[]{:S(2)}, u32[]{:S(2)}) collective-permute-start(bf16[2,7,8,2560]{3,2,1,0:T(8,128)(2,1)S(1)} %collective-permute-done.refs_2_), channel_id=1, source_target_pairs={{0,1},{1,0},{2,3},{3,2},{4,5},{5,4},{6,7},{7,6},{8,9},{9,8},{10,11... | collective-permute-start | bytes 1720328 | tf_op jit(solution)/shard_map/ppermute | solution.py:340
  277.1 2.4 collective-permute-start.5

commit v6 on v5

--- a/solution.py
+++ b/solution.py
@@ -31,7 +31,7 @@
     g, w, m_in, v_in, out, m, v = (refs[i * units : (i + 1) * units] for i in range(7))
     after, refs = refs[7 * units : 7 * units + 2], refs[7 * units + 2 :]
     own, part, w_own = (refs[i * units : (i + 1) * units] for i in range(3))
-    own_sem, state_sem, across_send, push_recv, ring_send, ring_recv, pass_recv, first_recv = refs[3 * units :]
+    across_send, ring_send, ring_recv, pass_recv = refs[3 * units :]
 
     me = lax.axis_index("dp")
     z, core = me // CORES, me % CORES
@@ -60,24 +60,11 @@
     def wait_bytes(ref, sem):
         pltpu.make_async_copy(ref, ref, sem).wait()
 
-    def load_own(k, u):
-        slot = lax.rem(k, 2)
-        for d in ways:
-            pltpu.make_async_copy(g[u].at[d, owner(d, k) * CORES + core], own[u].at[slot, d], own_sem.at[slot, u]).start()
-
     def push(d, k, u, sem, rows=slice(None)):
         pltpu.make_async_remote_copy(
             g[u].at[d, owner(d, k) * CORES + 1 - core, rows], part[u].at[d, k, rows], across_send.at[u], sem, **to(partner)
         ).start()
 
-    def push_all(k, u):
-        for d in ways:
-            push(d, k, u, push_recv.at[k, u])
-
-    def terms_here(k, u):
-        wait_bytes(own[u].at[lax.rem(k, 2)], own_sem.at[lax.rem(k, 2), u])
-        wait_bytes(part[u].at[:, k], push_recv.at[k, u])
-
     def send(block, d, t, u, rows=slice(None), sem=None):
         piece = out[u].at[d, block, rows]
         sem = ring_recv.at[lax.rem(t, 3), d, u] if sem is None else sem
@@ -98,91 +85,108 @@
 
     rows_of = [x.shape[2] for x in own]
 
-    for u in order:
-        load_own(0, u)
-
-    barrier = pltpu.get_barrier_semaphore()
-    for index in (chip(1) * CORES + core, chip(-1) * CORES + core, partner):
-        pl.semaphore_signal(barrier, inc=1, **to(index))
-    pl.semaphore_wait(barrier, 3)
-
-    for p, (at, count) in enumerate(cuts(rows_of[lead])):
-        for d in ways:
-            push(d, 0, lead, first_recv.at[d, p], pl.ds(at, count))
-    for u in others:
-        push_all(0, u)
-    for u in order:
-        load_own(1, u)
-        push_all(1, u)
-
-    def begin(d, u, at, count):
-        block = owner(d, 0) * CORES + core
-
-        @pl.loop(at, at + count)
-        def _(row):
-            out[u][d, block, row] = terms(0, d, 0, u, row).astype(out[u].dtype)
-
-        send(block, d, 0, u, pl.ds(at, count))
-
-    wait_bytes(own[lead].at[0], own_sem.at[0, lead])
-    for p, (at, count) in enumerate(cuts(rows_of[lead])):
-        for d in ways:
-            wait_bytes(part[lead].at[d, 0, pl.ds(at, count)], first_recv.at[d, p])
-            begin(d, lead, at, count)
-    for u in others:
-        terms_here(0, u)
-        for d in ways:
-            begin(d, u, 0, rows_of[u])
-
-    state = {}
-    for u in order:
-        state[u] = (
-            pltpu.make_async_copy(w[u].at[:, me], w_own[u], state_sem.at[0, u]),
-            pltpu.make_async_copy(m_in[u], m[u], state_sem.at[1, u]),
-            pltpu.make_async_copy(v_in[u], v[u], state_sem.at[2, u]),
-        )
-        for copy in state[u]:
-            copy.start()
-
-    @pl.loop(1, last)
-    def _(k):
-        slot = lax.rem(k, 2)
-        for u in order:
-            load_own(k + 1, u)
-            push_all(k + 1, u)
-        for u in order:
-            terms_here(k, u)
-            for d in ways:
-                block = owner(d, k) * CORES + core
-                arrived(block, d, k - 1, u)
+    def sums(own_sem, state_sem, push_recv, first_recv):
+        def load_own(k, u):
+            slot = lax.rem(k, 2)
+            for d in ways:
+                pltpu.make_async_copy(g[u].at[d, owner(d, k) * CORES + core], own[u].at[slot, d], own_sem.at[slot, u]).start()
+
+        def push_all(k, u):
+            for d in ways:
+                push(d, k, u, push_recv.at[k, u])
+
+        def terms_here(k, u):
+            wait_bytes(own[u].at[lax.rem(k, 2)], own_sem.at[lax.rem(k, 2), u])
+            wait_bytes(part[u].at[:, k], push_recv.at[k, u])
+
+        for u in order:
+            load_own(0, u)
+
+        barrier = pltpu.get_barrier_semaphore()
+        for index in (chip(1) * CORES + core, chip(-1) * CORES + core, partner):
+            pl.semaphore_signal(barrier, inc=1, **to(index))
+        pl.semaphore_wait(barrier, 3)
+
+        for p, (at, count) in enumerate(cuts(rows_of[lead])):
+            for d in ways:
+                push(d, 0, lead, first_recv.at[d, p], pl.ds(at, count))
+        for u in others:
+            push_all(0, u)
+        for u in order:
+            load_own(1, u)
+            push_all(1, u)
+
+        def begin(d, u, at, count):
+            block = owner(d, 0) * CORES + core
+
+            @pl.loop(at, at + count)
+            def _(row):
+                out[u][d, block, row] = terms(0, d, 0, u, row).astype(out[u].dtype)
+
+            send(block, d, 0, u, pl.ds(at, count))
+
+        wait_bytes(own[lead].at[0], own_sem.at[0, lead])
+        for p, (at, count) in enumerate(cuts(rows_of[lead])):
+            for d in ways:
+                wait_bytes(part[lead].at[d, 0, pl.ds(at, count)], first_recv.at[d, p])
+                begin(d, lead, at, count)
+        for u in others:
+            terms_here(0, u)
+            for d in ways:
+                begin(d, u, 0, rows_of[u])
+
+        state = {}
+        for u in order:
+            state[u] = (
+                pltpu.make_async_copy(w[u].at[:, me], w_own[u], state_sem.at[0, u]),
+                pltpu.make_async_copy(m_in[u], m[u], state_sem.at[1, u]),
+                pltpu.make_async_copy(v_in[u], v[u], state_sem.at[2, u]),
+            )
+            for copy in state[u]:
+                copy.start()
+
+        @pl.loop(1, last)
+        def _(k):
+            slot = lax.rem(k, 2)
+            for u in order:
+                load_own(k + 1, u)
+                push_all(k + 1, u)
+            for u in order:
+                terms_here(k, u)
+                for d in ways:
+                    block = owner(d, k) * CORES + core
+                    arrived(block, d, k - 1, u)
+
+                    @pl.loop(0, rows_of[u])
+                    def _(row):
+                        total = out[u][d, block, row].astype(jnp.float32) + terms(slot, d, k, u, row)
+                        out[u][d, block, row] = total.astype(out[u].dtype)
+
+                    if d == 0:
+                        sent(u)
+                    send(block, d, k, u)
+
+        for u in order:
+            terms_here(last, u)
+            for copy in state[u]:
+                copy.wait()
+            for d in ways:
+                arrived(me, d, last - 1, u)
 
                 @pl.loop(0, rows_of[u])
                 def _(row):
-                    total = out[u][d, block, row].astype(jnp.float32) + terms(slot, d, k, u, row)
-                    out[u][d, block, row] = total.astype(out[u].dtype)
+                    total = out[u][d, me, row].astype(jnp.float32) + terms(last % 2, d, last, u, row)
+                    gradient = total.astype(jnp.bfloat16).astype(jnp.float32)
+                    new = adamw(w_own[u][d, row].astype(jnp.float32), m[u][d, row], v[u][d, row], gradient)
+                    out[u][d, me, row], m[u][d, row], v[u][d, row] = new
 
                 if d == 0:
                     sent(u)
-                send(block, d, k, u)
-
-    for u in order:
-        terms_here(last, u)
-        for copy in state[u]:
-            copy.wait()
-        for d in ways:
-            arrived(me, d, last - 1, u)
-
-            @pl.loop(0, rows_of[u])
-            def _(row):
-                total = out[u][d, me, row].astype(jnp.float32) + terms(last % 2, d, last, u, row)
-                gradient = total.astype(jnp.bfloat16).astype(jnp.float32)
-                new = adamw(w_own[u][d, row].astype(jnp.float32), m[u][d, row], v[u][d, row], gradient)
-                out[u][d, me, row], m[u][d, row], v[u][d, row] = new
-
-            if d == 0:
-                sent(u)
-            send(me, d, last, u)
-            pass_on(me, d, u)
+                send(me, d, last, u)
+                pass_on(me, d, u)
+
+    dma = lambda *shape: pltpu.SemaphoreType.DMA(shape)
+    pl.run_scoped(sums, dma(2, units), dma(3, units), dma(ring, units), dma(2, len(cuts(rows_of[lead]))))
 
     def forward(d, j, u):
         block = behind(d, j) * CORES + core
@@ -289,14 +293,10 @@
                 *(pltpu.VMEM((2, 2, *b), jnp.bfloat16) for b in block),
                 *(pltpu.VMEM((2, ring, *b), jnp.bfloat16) for b in block),
                 *(pltpu.VMEM((2, *b), jnp.bfloat16) for b in block),
-                dma(2, units),
-                dma(3, units),
                 dma(units),
-                dma(ring, units),
                 dma(units),
                 dma(3, 2, units),
                 dma(units),
-                dma(2, 3),
             ],
             compiler_params=pltpu.CompilerParams(collective_id=0, has_side_effects=True, vmem_limit_bytes=VMEM_LIMIT),
             name="step_end",

time: 281 us -> 280 us (level)
  no operation moved by 1% of the time
where the time goes in v6:
time: 280 us
  Pallas kernels  271 us (97%)
  starting transfers between devices  4.2 us (2%)
  waiting for transfers between devices  3.99 us (1%)
    pallas_call x1, Pallas kernels, whole_step(): pl.pallas_call(functools.partial(kernel, n, order, late), out_shape=[*(pl...  257 us
    pallas_call x1, Pallas kernels, whole_step(): writer(*(pltpu.with_memory_space_constraint(x, pltpu.VMEM) for x in new))  11.3 us
  transfers between devices with their start and end apart: 6, of which 4 were waited for; matrix products, arithmetic and copies ran while one was open for 0% of the time, Pallas kernels for 5%

profile of v6, /device:TPU:21, one launch (start us, length us, event | category | flops | bytes accessed | tf_op | source)
XLA Modules:
  0.0 280.2 jit_solution(12882241633375850935)
XLA Ops:
  0.6 257.4 %step_end.1 = (bf16[2,16,7,8,2560]{4,3,2,1,0:T(8,128)(2,1)S(1)}, bf16[2,16,7,8,2560]{4,3,2,1,0:T(8,128)(2,1)S(1)}, bf16[2,16,20,8,896]{4,3,2,1,0:T(8,128)(2,1)S(...) custom-call(bf16[2,16,7,8,2560]{4,3,2,1,0:T(8,128)(2,1)} %bitcast.23, ...), custom_call_target="tpu_custom_call" | custom-call | tf_op jit(solution)/shard_map/step_end/pallas_call | solution.py:284
  258.1 2.0 collective-permute-start.1
  260.1 0.0 collective-permute-start
  260.1 0.7 collective-permute-start.2
  260.8 0.0 collective-permute-start.3
  260.8 11.3 %place.1 = (bf16[2,16,7,8,2560]{4,3,2,1,0:T(8,128)(2,1)}, bf16[2,16,7,8,2560]{4,3,2,1,0:T(8,128)(2,1)}, bf16[2,16,20,8,896]{4,3,2,1,0:T(8,128)(2,1)}, f32[2,7,8,...) custom-call(bf16[2,16,7,8,2560]{4,3,2,1,0:T(8,128)(2,1)S(1)} %get-tu, ...), custom_call_target="tpu_custom_call" | custom-call | flops 3000000000 | bytes 40000000 | tf_op jit(solution)/shard_map/place/pallas_call | solution.py:320
  272.1 0.2 collective-permute-done.1.ref.refs_3_
  272.3 2.8 %collective-permute-done.refs_2_ = bf16[2,7,8,2560]{3,2,1,0:T(8,128)(2,1)S(1)} collective-permute-done((bf16[2,7,8,2560]{3,2,1,0:T(8,128)(2,1)S(1)}, bf16[2,7,8,2560]{3,2,1,0:T(8,128)(2,1)S(1)}, u32[]{:S(2)}, u32[]{:S(2)}) %collective-permute-start) | collective-permute-done | bytes 573472 | tf_op jit(solution)/shard_map/ppermute | solution.py:308
  275.2 1.5 collective-permute-start.4
  276.7 0.0 collective-permute-start.5
  276.7 0.0 collective-permute-done.2.refs_4_
  276.7 0.0 collective-permute-done.3.refs_5_
  276.7 1.5 put.2
  278.2 0.1 collective-permute-done.4.refs_2_
  278.3 0.8 collective-permute-done.5.refs_3_
  279.1 1.0 put.3
  (1 shorter events, 0.0 us)
Async XLA Ops:
  258.1 14.2 %collective-permute-start.1 = (bf16[2,7,8,2560]{3,2,1,0:T(8,128)(2,1)S(1)}, bf16[2,7,8,2560]{3,2,1,0:T(8,128)(2,1)S(1)}, u32[]{:S(2)}, u32[]{:S(2)}) collective-permute-start(bf16[2,7,8,2560]{3,2,1,0:T(8,128)(2,1)S(1)} %get-tuple-element.40), channel_id=1, source_target_pairs={{0,14},{1,15},{2,0},{3,1},{4,2},{5,3},{6,4},{7,5},{8,6},{9,7},{10,... | collective-permute-start | bytes 1720328 | tf_op jit(solution)/shard_map/ppermute | solution.py:308
  260.1 15.1 %collective-permute-start = (bf16[2,7,8,2560]{3,2,1,0:T(8,128)(2,1)S(1)}, bf16[2,7,8,2560]{3,2,1,0:T(8,128)(2,1)S(1)}, u32[]{:S(2)}, u32[]{:S(2)}) collective-permute-start(bf16[2,7,8,2560]{3,2,1,0:T(8,128)(2,1)S(1)} %get-tuple-element.39), channel_id=1, source_target_pairs={{0,2},{1,3},{2,4},{3,5},{4,6},{5,7},{6,8},{7,9},{8,10},{9,11},{10,... | collective-permute-start | bytes 1720328 | tf_op jit(solution)/shard_map/ppermute | solution.py:308
  260.1 16.6 %collective-permute-start.2 = (bf16[2,7,8,2560]{3,2,1,0:T(8,128)(2,1)S(1)}, bf16[2,7,8,2560]{3,2,1,0:T(8,128)(2,1)S(1)}, u32[]{:S(2)}, u32[]{:S(2)}) collective-permute-start(bf16[2,7,8,2560]{3,2,1,0:T(8,128)(2,1)S(1)} %get-tuple-element.39), channel_id=1, source_target_pairs={{0,1},{1,0},{2,3},{3,2},{4,5},{5,4},{6,7},{7,6},{8,9},{9,8},{10,11... | collective-permute-start | bytes 1720328 | tf_op jit(solution)/shard_map/ppermute | solution.py:309
  260.8 15.9 %collective-permute-start.3 = (bf16[2,7,8,2560]{3,2,1,0:T(8,128)(2,1)S(1)}, bf16[2,7,8,2560]{3,2,1,0:T(8,128)(2,1)S(1)}, u32[]{:S(2)}, u32[]{:S(2)}) collective-permute-start(bf16[2,7,8,2560]{3,2,1,0:T(8,128)(2,1)S(1)} %get-tuple-element.40), channel_id=1, source_target_pairs={{0,1},{1,0},{2,3},{3,2},{4,5},{5,4},{6,7},{7,6},{8,9},{9,8},{10,11... | collective-permute-start | bytes 1720328 | tf_op jit(solution)/shard_map/ppermute | solution.py:309
  275.2 3.1 %collective-permute-start.4 = (bf16[2,7,8,2560]{3,2,1,0:T(8,128)(2,1)S(1)}, bf16[2,7,8,2560]{3,2,1,0:T(8,128)(2,1)S(1)}, u32[]{:S(2)}, u32[]{:S(2)}) collective-permute-start(bf16[2,7,8,2560]{3,2,1,0:T(8,128)(2,1)S(1)} %collective-permute-done.refs_2_), channel_id=1, source_target_pairs={{0,1},{1,0},{2,3},{3,2},{4,5},{5,4},{6,7},{7,6},{8,9},{9,8},{10,11... | collective-permute-start | bytes 1720328 | tf_op jit(solution)/shard_map/ppermute | solution.py:340
  276.7 2.4 collective-permute-start.5

commit v7 on v6

--- a/solution.py
+++ b/solution.py
@@ -10,6 +10,7 @@
 
 CORES = 2
 SUBLANES = 8
+SHORT = 2
 VMEM_LIMIT = 20 * 2**20
 
 
@@ -31,7 +32,7 @@
     g, w, m_in, v_in, out, m, v = (refs[i * units : (i + 1) * units] for i in range(7))
     after, refs = refs[7 * units : 7 * units + 2], refs[7 * units + 2 :]
     own, part, w_own = (refs[i * units : (i + 1) * units] for i in range(3))
-    across_send, ring_send, ring_recv, pass_recv = refs[3 * units :]
+    across_send, ring_send, ring_recv, pass_recv, short_sem = refs[3 * units :]
 
     me = lax.axis_index("dp")
     z, core = me // CORES, me % CORES
@@ -188,15 +189,25 @@
     dma = lambda *shape: pltpu.SemaphoreType.DMA(shape)
     pl.run_scoped(sums, dma(2, units), dma(3, units), dma(ring, units), dma(2, len(cuts(rows_of[lead]))))
 
-    def forward(d, j, u):
+    rest = pl.ds(SHORT, rows_of[lead] - SHORT)
+
+    def forward(d, j, u, rows=slice(None)):
         block = behind(d, j) * CORES + core
         arrived(block, d, last + j - 1, u)
         if d == 0:
             sent(u)
-        send(block, d, last + j, u)
+        send(block, d, last + j, u, rows)
         pass_on(block, d, u)
 
-    @pl.loop(1, last - 2)
+    for u in order:
+        for d in ways:
+            forward(d, 1, u)
+        if u == lead:
+            piece = out[u].at[0, me, pl.ds(0, SHORT)]
+            short = pltpu.make_async_remote_copy(piece, piece, short_sem.at[0], short_sem.at[1], **following(1))
+            short.start()
+
+    @pl.loop(2, last - 2)
     def _(j):
         for u in order:
             for d in ways:
@@ -205,7 +216,7 @@
     for u in order:
         if u == tail:
             for d in ways:
-                forward(d, last - 1, lead)
+                forward(d, last - 1, lead, slice(None) if d else rest)
         for d in ways:
             forward(d, last - 2, u)
 
@@ -213,7 +224,11 @@
         if u == tail:
             for d in ways:
                 block = behind(d, last) * CORES + core
-                arrived(block, d, 2 * last - 1, lead)
+                if d == 0:
+                    wait_bytes(out[lead].at[d, block, rest], ring_recv.at[(2 * last - 1) % 3, d, lead])
+                    wait_bytes(out[lead].at[d, block, pl.ds(0, SHORT)], short_sem.at[1])
+                else:
+                    arrived(block, d, 2 * last - 1, lead)
                 pass_on(block, d, lead)
         for d in ways:
             block = behind(d, last - 1) * CORES + core
@@ -223,8 +238,12 @@
             def _(row):
                 after[d][late.index(u), row] = out[u][d, block, row]
 
+    short.wait_send()
     for u in order:
-        sent(u)
+        if u == lead:
+            wait_bytes(out[u].at[0, pl.ds(0, 2), pl.ds(0, rows_of[u] - SHORT // 2)], ring_send.at[u])
+        else:
+            sent(u)
         passed = last - 1 if u in late else ring
         wait_bytes(out[u].at[:, pl.ds(0, ring + passed)], across_send.at[u])
         wait_bytes(out[u].at[:, pl.ds(0, passed)], pass_recv.at[u])
@@ -297,6 +316,7 @@
                 dma(units),
                 dma(3, 2, units),
                 dma(units),
+                dma(2),
             ],
             compiler_params=pltpu.CompilerParams(collective_id=0, has_side_effects=True, vmem_limit_bytes=VMEM_LIMIT),
             name="step_end",

time: 280 us -> 281 us (level)
  transfers between devices with their start and end apart: 6 -> 6, of which waited for: 4 -> 3; matrix products, arithmetic and copies ran while one was open for 0% -> 0% of each run, Pallas kernels for 5% -> 5%
where the time goes in v7:
time: 281 us
  Pallas kernels  271 us (96%)
  starting transfers between devices  5.43 us (2%)
  waiting for transfers between devices  3.97 us (1%)
    pallas_call x1, Pallas kernels, whole_step(): pl.pallas_call(functools.partial(kernel, n, order, late), out_shape=[*(pl...  257 us
    pallas_call x1, Pallas kernels, whole_step(): writer(*(pltpu.with_memory_space_constraint(x, pltpu.VMEM) for x in new))  11.3 us
  transfers between devices with their start and end apart: 6, of which 3 were waited for; matrix products, arithmetic and copies ran while one was open for 0% of the time, Pallas kernels for 5%

profile of v7, /device:TPU:21, one launch (start us, length us, event | category | flops | bytes accessed | tf_op | source)
XLA Modules:
  0.0 280.8 jit_solution(15336817041916586507)
XLA Ops:
  0.6 256.9 %step_end.1 = (bf16[2,16,7,8,2560]{4,3,2,1,0:T(8,128)(2,1)S(1)}, bf16[2,16,7,8,2560]{4,3,2,1,0:T(8,128)(2,1)S(1)}, bf16[2,16,20,8,896]{4,3,2,1,0:T(8,128)(2,1)S(...) custom-call(bf16[2,16,7,8,2560]{4,3,2,1,0:T(8,128)(2,1)} %bitcast.23, ...), custom_call_target="tpu_custom_call" | custom-call | tf_op jit(solution)/shard_map/step_end/pallas_call | solution.py:303
  257.5 3.2 %collective-permute-start.1 = (bf16[2,7,8,2560]{3,2,1,0:T(8,128)(2,1)S(1)}, bf16[2,7,8,2560]{3,2,1,0:T(8,128)(2,1)S(1)}, u32[]{:S(2)}, u32[]{:S(2)}) collective-permute-start(bf16[2,7,8,2560]{3,2,1,0:T(8,128)(2,1)S(1)} %get-tuple-element.40), channel_id=1, source_target_pairs={{0,14},{1,15},{2,0},{3,1},{4,2},{5,3},{6,4},{7,5},{8,6},{9,7},{10,... | collective-permute-start | bytes 1720328 | tf_op jit(solution)/shard_map/ppermute | solution.py:328
  260.7 0.0 collective-permute-start
  260.7 0.7 collective-permute-start.2
  261.4 0.0 collective-permute-start.3
  261.4 11.3 %place.1 = (bf16[2,16,7,8,2560]{4,3,2,1,0:T(8,128)(2,1)}, bf16[2,16,7,8,2560]{4,3,2,1,0:T(8,128)(2,1)}, bf16[2,16,20,8,896]{4,3,2,1,0:T(8,128)(2,1)}, f32[2,7,8,...) custom-call(bf16[2,16,7,8,2560]{4,3,2,1,0:T(8,128)(2,1)S(1)} %get-tu, ...), custom_call_target="tpu_custom_call" | custom-call | flops 3000000000 | bytes 40000000 | tf_op jit(solution)/shard_map/place/pallas_call | solution.py:340
  272.8 0.0 collective-permute-done.1.ref.refs_3_
  272.8 3.0 %collective-permute-done.refs_2_ = bf16[2,7,8,2560]{3,2,1,0:T(8,128)(2,1)S(1)} collective-permute-done((bf16[2,7,8,2560]{3,2,1,0:T(8,128)(2,1)S(1)}, bf16[2,7,8,2560]{3,2,1,0:T(8,128)(2,1)S(1)}, u32[]{:S(2)}, u32[]{:S(2)}) %collective-permute-start) | collective-permute-done | bytes 573472 | tf_op jit(solution)/shard_map/ppermute | solution.py:328
  275.8 1.5 collective-permute-start.4
  277.3 0.0 collective-permute-start.5
  277.3 0.0 collective-permute-done.2.refs_4_
  277.3 0.0 collective-permute-done.3.refs_5_
  277.3 1.5 put.2
  278.8 0.1 collective-permute-done.4.refs_2_
  278.9 0.8 collective-permute-done.5.refs_3_
  279.8 1.0 put.3
  (1 shorter events, 0.0 us)
Async XLA Ops:
  257.5 15.2 %collective-permute-start.1 = (bf16[2,7,8,2560]{3,2,1,0:T(8,128)(2,1)S(1)}, bf16[2,7,8,2560]{3,2,1,0:T(8,128)(2,1)S(1)}, u32[]{:S(2)}, u32[]{:S(2)}) collective-permute-start(bf16[2,7,8,2560]{3,2,1,0:T(8,128)(2,1)S(1)} %get-tuple-element.40), channel_id=1, source_target_pairs={{0,14},{1,15},{2,0},{3,1},{4,2},{5,3},{6,4},{7,5},{8,6},{9,7},{10,... | collective-permute-start | bytes 1720328 | tf_op jit(solution)/shard_map/ppermute | solution.py:328
  260.7 15.1 %collective-permute-start = (bf16[2,7,8,2560]{3,2,1,0:T(8,128)(2,1)S(1)}, bf16[2,7,8,2560]{3,2,1,0:T(8,128)(2,1)S(1)}, u32[]{:S(2)}, u32[]{:S(2)}) collective-permute-start(bf16[2,7,8,2560]{3,2,1,0:T(8,128)(2,1)S(1)} %get-tuple-element.39), channel_id=1, source_target_pairs={{0,2},{1,3},{2,4},{3,5},{4,6},{5,7},{6,8},{7,9},{8,10},{9,11},{10,... | collective-permute-start | bytes 1720328 | tf_op jit(solution)/shard_map/ppermute | solution.py:328
  260.7 16.6 %collective-permute-start.2 = (bf16[2,7,8,2560]{3,2,1,0:T(8,128)(2,1)S(1)}, bf16[2,7,8,2560]{3,2,1,0:T(8,128)(2,1)S(1)}, u32[]{:S(2)}, u32[]{:S(2)}) collective-permute-start(bf16[2,7,8,2560]{3,2,1,0:T(8,128)(2,1)S(1)} %get-tuple-element.39), channel_id=1, source_target_pairs={{0,1},{1,0},{2,3},{3,2},{4,5},{5,4},{6,7},{7,6},{8,9},{9,8},{10,11... | collective-permute-start | bytes 1720328 | tf_op jit(solution)/shard_map/ppermute | solution.py:329
  261.4 15.9 %collective-permute-start.3 = (bf16[2,7,8,2560]{3,2,1,0:T(8,128)(2,1)S(1)}, bf16[2,7,8,2560]{3,2,1,0:T(8,128)(2,1)S(1)}, u32[]{:S(2)}, u32[]{:S(2)}) collective-permute-start(bf16[2,7,8,2560]{3,2,1,0:T(8,128)(2,1)S(1)} %get-tuple-element.40), channel_id=1, source_target_pairs={{0,1},{1,0},{2,3},{3,2},{4,5},{5,4},{6,7},{7,6},{8,9},{9,8},{10,11... | collective-permute-start | bytes 1720328 | tf_op jit(solution)/shard_map/ppermute | solution.py:329
  275.8 3.1 %collective-permute-start.4 = (bf16[2,7,8,2560]{3,2,1,0:T(8,128)(2,1)S(1)}, bf16[2,7,8,2560]{3,2,1,0:T(8,128)(2,1)S(1)}, u32[]{:S(2)}, u32[]{:S(2)}) collective-permute-start(bf16[2,7,8,2560]{3,2,1,0:T(8,128)(2,1)S(1)} %collective-permute-done.refs_2_), channel_id=1, source_target_pairs={{0,1},{1,0},{2,3},{3,2},{4,5},{5,4},{6,7},{7,6},{8,9},{9,8},{10,11... | collective-permute-start | bytes 1720328 | tf_op jit(solution)/shard_map/ppermute | solution.py:360
  277.3 2.4 collective-permute-start.5

commit v8 on v6

v8 whole, which is shorter than its diff:
```python
import functools

import jax
import jax.numpy as jnp
from jax import lax
from jax.experimental import pallas as pl
from jax.experimental.pallas import tpu as pltpu
from jax.sharding import PartitionSpec as P


CORES = 2
SUBLANES = 8
SHORT = 2
VMEM_LIMIT = 20 * 2**20


def adamw(w, m, v, g):
    m = 0.9 * m + 0.1 * g
    v = 0.95 * v + 0.05 * g * g
    step = m * lax.rsqrt(v + 1e-8) + 0.1 * w
    return (w - 0.02 * step).astype(jnp.bfloat16), m, v


def cuts(rows):
    a = max(rows // 8, 1)
    b = max(rows // 3, a + 1)
    return (0, a), (a, b - a), (b, rows - b)


def kernel(n, order, late, *refs):
    units = len(order)
    g, w, m_in, v_in, out, m, v = (refs[i * units : (i + 1) * units] for i in range(7))
    after, refs = refs[7 * units : 7 * units + 2], refs[7 * units + 2 :]
    own, part, w_own = (refs[i * units : (i + 1) * units] for i in range(3))
    last_send, last_recv = refs[3 * units :]

    me = lax.axis_index("dp")
    z, core = me // CORES, me % CORES
    ring = n // CORES
    partner = z * CORES + 1 - core
    last = ring - 1
    ways = (0, 1)
    lead, *others = order
    tail = order[-1]
    rows_of = [x.shape[2] for x in own]

    def chip(offset):
        return lax.rem(z + offset + 2 * ring, ring)

    def behind(d, j):
        return chip(j if d else -j)

    def owner(d, k):
        return behind(d, k + 1)

    def to(index):
        return {"device_id": {"dp": index}, "device_id_type": pl.DeviceIdType.MESH}

    def following(d):
        return to(behind(d, -1) * CORES + core)

    def wait_bytes(ref, sem):
        pltpu.make_async_copy(ref, ref, sem).wait()

    def hand_over(d, u):
        block = behind(d, last - 1) * CORES + core

        @pl.loop(0, rows_of[u])
        def _(row):
            after[d][late.index(u), row] = out[u][d, block, row]

    dma = lambda *shape: pltpu.SemaphoreType.DMA(shape)

    def rings(across_send, ring_send, ring_recv, pass_recv, short_sem):
        def push(d, k, u, sem, rows=slice(None)):
            pltpu.make_async_remote_copy(
                g[u].at[d, owner(d, k) * CORES + 1 - core, rows], part[u].at[d, k, rows], across_send.at[u], sem, **to(partner)
            ).start()

        def send(block, d, t, u, rows=slice(None)):
            piece = out[u].at[d, block, rows]
            closing = u == tail and isinstance(t, int) and t == 2 * last - 2
            sems = (last_send, last_recv.at[d]) if closing else (ring_send.at[u], ring_recv.at[lax.rem(t, 3), d, u])
            pltpu.make_async_remote_copy(piece, piece, *sems, **following(d)).start()

        def sent(u):
            wait_bytes(out[u].at[:, 0], ring_send.at[u])

        def arrived(block, d, t, u):
            wait_bytes(out[u].at[d, block], ring_recv.at[lax.rem(t, 3), d, u])

        def pass_on(block, d, u, rows=slice(None)):
            piece = out[u].at[d, block, rows]
            pltpu.make_async_remote_copy(piece, piece, across_send.at[u], pass_recv.at[u], **to(partner)).start()

        def terms(slot, d, k, u, row):
            return own[u][slot, d, row].astype(jnp.float32) + part[u][d, k, row].astype(jnp.float32)

        def sums(own_sem, state_sem, push_recv, first_recv):
            def load_own(k, u):
                slot = lax.rem(k, 2)
                for d in ways:
                    pltpu.make_async_copy(g[u].at[d, owner(d, k) * CORES + core], own[u].at[slot, d], own_sem.at[slot, u]).start()

            def push_all(k, u):
                for d in ways:
                    push(d, k, u, push_recv.at[k, u])

            def terms_here(k, u):
                wait_bytes(own[u].at[lax.rem(k, 2)], own_sem.at[lax.rem(k, 2), u])
                wait_bytes(part[u].at[:, k], push_recv.at[k, u])

            for u in order:
                load_own(0, u)

            barrier = pltpu.get_barrier_semaphore()
            for index in (chip(1) * CORES + core, chip(-1) * CORES + core, partner):
                pl.semaphore_signal(barrier, inc=1, **to(index))
            pl.semaphore_wait(barrier, 3)

            for p, (at, count) in enumerate(cuts(rows_of[lead])):
                for d in ways:
                    push(d, 0, lead, first_recv.at[d, p], pl.ds(at, count))
            for u in others:
                push_all(0, u)
            for u in order:
                load_own(1, u)
                push_all(1, u)

            def begin(d, u, at, count):
                block = owner(d, 0) * CORES + core

                @pl.loop(at, at + count)
                def _(row):
                    out[u][d, block, row] = terms(0, d, 0, u, row).astype(out[u].dtype)

                send(block, d, 0, u, pl.ds(at, count))

            wait_bytes(own[lead].at[0], own_sem.at[0, lead])
            for p, (at, count) in enumerate(cuts(rows_of[lead])):
                for d in ways:
                    wait_bytes(part[lead].at[d, 0, pl.ds(at, count)], first_recv.at[d, p])
                    begin(d, lead, at, count)
            for u in others:
                terms_here(0, u)
                for d in ways:
                    begin(d, u, 0, rows_of[u])

            state = {}
            for u in order:
                state[u] = (
                    pltpu.make_async_copy(w[u].at[:, me], w_own[u], state_sem.at[0, u]),
                    pltpu.make_async_copy(m_in[u], m[u], state_sem.at[1, u]),
                    pltpu.make_async_copy(v_in[u], v[u], state_sem.at[2, u]),
                )
                for copy in state[u]:
                    copy.start()

            @pl.loop(1, last)
            def _(k):
                slot = lax.rem(k, 2)
                for u in order:
                    load_own(k + 1, u)
                    push_all(k + 1, u)
                for u in order:
                    terms_here(k, u)
                    for d in ways:
                        block = owner(d, k) * CORES + core
                        arrived(block, d, k - 1, u)

                        @pl.loop(0, rows_of[u])
                        def _(row):
                            total = out[u][d, block, row].astype(jnp.float32) + terms(slot, d, k, u, row)
                            out[u][d, block, row] = total.astype(out[u].dtype)

                        if d == 0:
                            sent(u)
                        send(block, d, k, u)

            for u in order:
                terms_here(last, u)
                for copy in state[u]:
                    copy.wait()
                for d in ways:
                    arrived(me, d, last - 1, u)

                    @pl.loop(0, rows_of[u])
                    def _(row):
                        total = out[u][d, me, row].astype(jnp.float32) + terms(last % 2, d, last, u, row)
                        gradient = total.astype(jnp.bfloat16).astype(jnp.float32)
                        new = adamw(w_own[u][d, row].astype(jnp.float32), m[u][d, row], v[u][d, row], gradient)
                        out[u][d, me, row], m[u][d, row], v[u][d, row] = new

                    if d == 0:
                        sent(u)
                    send(me, d, last, u)
                    pass_on(me, d, u)

        pl.run_scoped(sums, dma(2, units), dma(3, units), dma(ring, units), dma(2, len(cuts(rows_of[lead]))))

        rest = pl.ds(SHORT, rows_of[lead] - SHORT)

        def forward(d, j, u, rows=slice(None)):
            block = behind(d, j) * CORES + core
            arrived(block, d, last + j - 1, u)
            if d == 0:
                sent(u)
            send(block, d, last + j, u, rows)
            pass_on(block, d, u)

        for u in order:
            for d in ways:
                forward(d, 1, u)
            if u == lead:
                piece = out[u].at[0, me, pl.ds(0, SHORT)]
                short = pltpu.make_async_remote_copy(piece, piece, short_sem.at[0], short_sem.at[1], **following(1))
                short.start()

        @pl.loop(2, last - 2)
        def _(j):
            for u in order:
                for d in ways:
                    forward(d, j, u)

        for u in order:
            if u == tail:
                for d in ways:
                    forward(d, last - 1, lead, slice(None) if d else rest)
            for d in ways:
                forward(d, last - 2, u)

        for u in others[:-1]:
            for d in ways:
                arrived(behind(d, last - 1) * CORES + core, d, 2 * last - 2, u)
                hand_over(d, u)
        block = behind(0, last) * CORES + core
        wait_bytes(out[lead].at[0, block, rest], ring_recv.at[(2 * last - 1) % 3, 0, lead])
        wait_bytes(out[lead].at[0, block, pl.ds(0, SHORT)], short_sem.at[1])
        pass_on(block, 0, lead)
        block = behind(1, last) * CORES + core
        arrived(block, 1, 2 * last - 1, lead)
        pass_on(block, 1, lead)

        short.wait_send()
        for u in order:
            if u == lead:
                wait_bytes(out[u].at[0, pl.ds(0, 2), pl.ds(0, rows_of[u] - SHORT // 2)], ring_send.at[u])
            elif u != tail:
                sent(u)
            passed = last - 1 if u in late else ring
            wait_bytes(out[u].at[:, pl.ds(0, ring + passed)], across_send.at[u])
            wait_bytes(out[u].at[:, pl.ds(0, passed)], pass_recv.at[u])

    pl.run_scoped(rings, dma(units), dma(units), dma(3, 2, units), dma(units), dma(2))

    for d in ways[::-1]:
        wait_bytes(out[tail].at[d, behind(d, last - 1) * CORES + core], last_recv.at[d])
        hand_over(d, tail)
    wait_bytes(out[tail].at[:, 0], last_send)


def place(*refs):
    count = (len(refs) - 1) // 2
    copies = [pltpu.make_async_copy(refs[i], refs[count + i], refs[-1].at[i]) for i in range(count)]
    for copy in copies:
        copy.start()
    for copy in copies:
        copy.wait()


def put(n, late, where, *refs):
    count = len(late)
    blocks, out, sem = refs[count : count + len(where)], refs[-1 - count : -1], refs[-1]
    me = lax.axis_index("dp")
    z, core = me // CORES, me % CORES
    ring = n // CORES
    copies = []
    for part, (d, back, partners) in zip(blocks, where, strict=True):
        index = lax.rem(z + (back if d else ring - back), ring) * CORES + (1 - core if partners else core)
        copies += [pltpu.make_async_copy(part.at[i], out[i].at[d, index], sem.at[len(copies) + i]) for i in range(count)]
    for copy in copies:
        copy.start()
    for copy in copies:
        copy.wait()


def marker(ref, out):
    out[...] = jnp.zeros_like(out)


def solution(mesh):
    n = mesh.shape["dp"]

    def step(*arrays):
        return whole_step(*arrays)

    def whole_step(*arrays):
        terms, weights, m, v = (arrays[i : i + 3] for i in (0, 3, 6, 9))
        units = len(terms)
        order, late = (2, 0, 1), (0, 1)
        layers = weights[0].shape[0]

        def blocks(x, count):
            return x.reshape(layers, *([count] if count else []), -1, SUBLANES, x.shape[-1])

        terms = [blocks(t[0], n) for t in terms]
        weights_in = [blocks(x, n) for x in weights]
        m_in = [blocks(x, 0) for x in m]
        v_in = [blocks(x, 0) for x in v]
        ring = n // CORES
        block = [x.shape[1:] for x in m_in]
        dma = lambda *shape: pltpu.SemaphoreType.DMA(shape)
        new = pl.pallas_call(
            functools.partial(kernel, n, order, late),
            out_shape=[
                *(pltpu.VMEM(x.shape, x.dtype) for x in (*weights_in, *m_in, *v_in)),
                *[pltpu.VMEM((len(late), *block[late[0]]), jnp.bfloat16)] * 2,
            ],
            in_specs=[pl.BlockSpec(memory_space=pltpu.HBM)] * (4 * units),
            out_specs=[pl.BlockSpec(memory_space=pltpu.VMEM)] * (3 * units + 2),
            scratch_shapes=[
                *(pltpu.VMEM((2, 2, *b), jnp.bfloat16) for b in block),
                *(pltpu.VMEM((2, ring, *b), jnp.bfloat16) for b in block),
                *(pltpu.VMEM((2, *b), jnp.bfloat16) for b in block),
                pltpu.SemaphoreType.DMA,
                dma(2),
            ],
            compiler_params=pltpu.CompilerParams(collective_id=0, has_side_effects=True, vmem_limit_bytes=VMEM_LIMIT),
            name="step_end",
        )(*(pltpu.with_memory_space_constraint(x, pltpu.HBM) for x in (*terms, *weights_in, *m_in, *v_in)))
        new, after = new[: 3 * units], new[3 * units :]
        across = [(i, i ^ 1) for i in range(n)]
        far = []
        for d, way in enumerate((1, -1)):
            far.append(lax.ppermute(after[d], "dp", [(i, (i + way * CORES) % n) for i in range(n)]))
        near = [lax.ppermute(x, "dp", across) for x in after]
        writer = pl.pallas_call(
            place,
            out_shape=[jax.ShapeDtypeStruct(x.shape, x.dtype) for x in new],
            in_specs=[pl.BlockSpec(memory_space=pltpu.VMEM)] * len(new),
            out_specs=[pl.BlockSpec(memory_space=pltpu.HBM)] * len(new),
            scratch_shapes=[dma(len(new))],
            compiler_params=pltpu.CompilerParams(vmem_limit_bytes=VMEM_LIMIT),
            name="place",
            cost_estimate=pl.CostEstimate(flops=3 * 10**9, bytes_accessed=4 * 10**7, transcendentals=0),
        )
        new = list(writer(*(pltpu.with_memory_space_constraint(x, pltpu.VMEM) for x in new)))
        last = n // CORES - 1

        def write(parts, where):
            done = pl.pallas_call(
                functools.partial(put, n, late, where),
                out_shape=[jax.ShapeDtypeStruct(new[u].shape, new[u].dtype) for u in late],
                in_specs=[pl.BlockSpec(memory_space=pltpu.HBM)] * len(late) + [pl.BlockSpec(memory_space=pltpu.VMEM)] * len(parts),
                out_specs=[pl.BlockSpec(memory_space=pltpu.HBM)] * len(late),
                scratch_shapes=[dma(len(where) * len(late))],
                input_output_aliases={i: i for i in range(len(late))},
                compiler_params=pltpu.CompilerParams(vmem_limit_bytes=VMEM_LIMIT),
                cost_estimate=pl.CostEstimate(flops=2 * 10**8, bytes_accessed=2 * 10**6, transcendentals=0),
                name="put",
            )(*(new[u] for u in late), *(pltpu.with_memory_space_constraint(x, pltpu.VMEM) for x in parts))
            for u, x in zip(late, done, strict=True):
                new[u] = x

        def swap(d):
            far[d], new[late[0]] = lax.optimization_barrier((far[d], new[late[0]]))
            return lax.ppermute(far[d], "dp", across)

        swapped = {1: swap(1)}
        mark = pl.pallas_call(
            marker,
            out_shape=pltpu.VMEM((SUBLANES, 128), jnp.float32),
            in_specs=[pl.BlockSpec(memory_space=pltpu.VMEM)],
            out_specs=pl.BlockSpec(memory_space=pltpu.VMEM),
            compiler_params=pltpu.CompilerParams(vmem_limit_bytes=VMEM_LIMIT),
            cost_estimate=pl.CostEstimate(flops=10**5, bytes_accessed=10**4, transcendentals=0),
            name="mark",
        )(far[1])
        far[0], mark = lax.optimization_barrier((far[0], mark))
        swapped[0] = swap(0)
        write((*far, *near, mark), ((0, last, 0), (1, last, 0), (0, last - 1, 1), (1, last - 1, 1)))
        write((swapped[0], swapped[1]), ((0, last, 1), (1, last, 1)))
        return tuple(x.reshape(like.shape) for x, like in zip(new, (*weights, *m, *v), strict=True))

    all_of, cut = P(None, None, None), P(None, "dp", None)
    step = jax.shard_map(
        step,
        mesh=mesh,
        in_specs=(P(("rep", "dp"), None, None, None),) * 3 + (all_of,) * 3 + (cut,) * 6,
        out_specs=(P("rep", None, None),) * 3 + (P("rep", "dp", None),) * 6,
        check_vma=False,
    )
    return step
```

time: 280 us -> 281 us (level)
  transfers between devices with their start and end apart: 6 -> 6, of which waited for: 4 -> 3; matrix products, arithmetic and copies ran while one was open for 0% -> 0% of each run, Pallas kernels for 5% -> 5%
where the time goes in v8:
time: 281 us
  Pallas kernels  270 us (96%)
  starting transfers between devices  5.55 us (2%)
  waiting for transfers between devices  3.97 us (1%)
    pallas_call x1, Pallas kernels, whole_step(): pl.pallas_call(functools.partial(kernel, n, order, late), out_shape=[*(pl...  257 us
    pallas_call x1, Pallas kernels, whole_step(): writer(*(pltpu.with_memory_space_constraint(x, pltpu.VMEM) for x in new))  11.3 us
  transfers between devices with their start and end apart: 6, of which 3 were waited for; matrix products, arithmetic and copies ran while one was open for 0% of the time, Pallas kernels for 5%

profile of v8, /device:TPU:21, one launch (start us, length us, event | category | flops | bytes accessed | tf_op | source)
XLA Modules:
  0.0 280.6 jit_solution(17522446218727441297)
XLA Ops:
  0.6 256.6 %step_end.1 = (bf16[2,16,7,8,2560]{4,3,2,1,0:T(8,128)(2,1)S(1)}, bf16[2,16,7,8,2560]{4,3,2,1,0:T(8,128)(2,1)S(1)}, bf16[2,16,20,8,896]{4,3,2,1,0:T(8,128)(2,1)S(...) custom-call(bf16[2,16,7,8,2560]{4,3,2,1,0:T(8,128)(2,1)} %bitcast.23, ...), custom_call_target="tpu_custom_call" | custom-call | tf_op jit(solution)/shard_map/step_end/pallas_call | solution.py:313
  257.2 3.3 %collective-permute-start.1 = (bf16[2,7,8,2560]{3,2,1,0:T(8,128)(2,1)S(1)}, bf16[2,7,8,2560]{3,2,1,0:T(8,128)(2,1)S(1)}, u32[]{:S(2)}, u32[]{:S(2)}) collective-permute-start(bf16[2,7,8,2560]{3,2,1,0:T(8,128)(2,1)S(1)} %get-tuple-element.40), channel_id=1, source_target_pairs={{0,14},{1,15},{2,0},{3,1},{4,2},{5,3},{6,4},{7,5},{8,6},{9,7},{10,... | collective-permute-start | bytes 1720328 | tf_op jit(solution)/shard_map/ppermute | solution.py:335
  260.5 0.0 collective-permute-start
  260.5 0.7 collective-permute-start.2
  261.2 0.0 collective-permute-start.3
  261.2 11.3 %place.1 = (bf16[2,16,7,8,2560]{4,3,2,1,0:T(8,128)(2,1)}, bf16[2,16,7,8,2560]{4,3,2,1,0:T(8,128)(2,1)}, bf16[2,16,20,8,896]{4,3,2,1,0:T(8,128)(2,1)}, f32[2,7,8,...) custom-call(bf16[2,16,7,8,2560]{4,3,2,1,0:T(8,128)(2,1)S(1)} %get-tu, ...), custom_call_target="tpu_custom_call" | custom-call | flops 3000000000 | bytes 40000000 | tf_op jit(solution)/shard_map/place/pallas_call | solution.py:347
  272.6 0.0 collective-permute-done.1.ref.refs_3_
  272.6 3.0 %collective-permute-done.refs_2_ = bf16[2,7,8,2560]{3,2,1,0:T(8,128)(2,1)S(1)} collective-permute-done((bf16[2,7,8,2560]{3,2,1,0:T(8,128)(2,1)S(1)}, bf16[2,7,8,2560]{3,2,1,0:T(8,128)(2,1)S(1)}, u32[]{:S(2)}, u32[]{:S(2)}) %collective-permute-start) | collective-permute-done | bytes 573472 | tf_op jit(solution)/shard_map/ppermute | solution.py:335
  275.6 1.5 collective-permute-start.4
  277.1 0.0 collective-permute-start.5
  277.2 0.0 collective-permute-done.2.refs_4_
  277.2 0.0 collective-permute-done.3.refs_5_
  277.2 1.5 put.2
  278.6 0.1 collective-permute-done.4.refs_2_
  278.8 0.8 collective-permute-done.5.refs_3_
  279.6 1.0 put.3
  (1 shorter events, 0.0 us)
Async XLA Ops:
  257.2 15.4 %collective-permute-start.1 = (bf16[2,7,8,2560]{3,2,1,0:T(8,128)(2,1)S(1)}, bf16[2,7,8,2560]{3,2,1,0:T(8,128)(2,1)S(1)}, u32[]{:S(2)}, u32[]{:S(2)}) collective-permute-start(bf16[2,7,8,2560]{3,2,1,0:T(8,128)(2,1)S(1)} %get-tuple-element.40), channel_id=1, source_target_pairs={{0,14},{1,15},{2,0},{3,1},{4,2},{5,3},{6,4},{7,5},{8,6},{9,7},{10,... | collective-permute-start | bytes 1720328 | tf_op jit(solution)/shard_map/ppermute | solution.py:335
  260.5 15.1 %collective-permute-start = (bf16[2,7,8,2560]{3,2,1,0:T(8,128)(2,1)S(1)}, bf16[2,7,8,2560]{3,2,1,0:T(8,128)(2,1)S(1)}, u32[]{:S(2)}, u32[]{:S(2)}) collective-permute-start(bf16[2,7,8,2560]{3,2,1,0:T(8,128)(2,1)S(1)} %get-tuple-element.39), channel_id=1, source_target_pairs={{0,2},{1,3},{2,4},{3,5},{4,6},{5,7},{6,8},{7,9},{8,10},{9,11},{10,... | collective-permute-start | bytes 1720328 | tf_op jit(solution)/shard_map/ppermute | solution.py:335
  260.5 16.6 %collective-permute-start.2 = (bf16[2,7,8,2560]{3,2,1,0:T(8,128)(2,1)S(1)}, bf16[2,7,8,2560]{3,2,1,0:T(8,128)(2,1)S(1)}, u32[]{:S(2)}, u32[]{:S(2)}) collective-permute-start(bf16[2,7,8,2560]{3,2,1,0:T(8,128)(2,1)S(1)} %get-tuple-element.39), channel_id=1, source_target_pairs={{0,1},{1,0},{2,3},{3,2},{4,5},{5,4},{6,7},{7,6},{8,9},{9,8},{10,11... | collective-permute-start | bytes 1720328 | tf_op jit(solution)/shard_map/ppermute | solution.py:336
  261.2 15.9 %collective-permute-start.3 = (bf16[2,7,8,2560]{3,2,1,0:T(8,128)(2,1)S(1)}, bf16[2,7,8,2560]{3,2,1,0:T(8,128)(2,1)S(1)}, u32[]{:S(2)}, u32[]{:S(2)}) collective-permute-start(bf16[2,7,8,2560]{3,2,1,0:T(8,128)(2,1)S(1)} %get-tuple-element.40), channel_id=1, source_target_pairs={{0,1},{1,0},{2,3},{3,2},{4,5},{5,4},{6,7},{7,6},{8,9},{9,8},{10,11... | collective-permute-start | bytes 1720328 | tf_op jit(solution)/shard_map/ppermute | solution.py:336
  275.6 3.1 %collective-permute-start.4 = (bf16[2,7,8,2560]{3,2,1,0:T(8,128)(2,1)S(1)}, bf16[2,7,8,2560]{3,2,1,0:T(8,128)(2,1)S(1)}, u32[]{:S(2)}, u32[]{:S(2)}) collective-permute-start(bf16[2,7,8,2560]{3,2,1,0:T(8,128)(2,1)S(1)} %collective-permute-done.refs_2_), channel_id=1, source_target_pairs={{0,1},{1,0},{2,3},{3,2},{4,5},{5,4},{6,7},{7,6},{8,9},{9,8},{10,11... | collective-permute-start | bytes 1720328 | tf_op jit(solution)/shard_map/ppermute | solution.py:367
  277.1 2.4 collective-permute-start.5
